TPU v7x, 256 devices: a whole 4x4x8 slice. The times are simulated.
256 devices in a mesh: blk: 32 (over z, y), rep: 8 (over x, core).
Axes of the slice: x: 4, y: 4, z: 8, core: 2. Of those that a mesh axis runs over, the one named last changes fastest.
Arguments:
- tensor_blocks: bfloat16 [512, 128, 128, 128], P(('blk', 'rep')), may hold values from -15 to 15
- triples: int32 [512, 3], P(('blk', 'rep')), may hold values from 0 to 63, as said below
- slot_count: int32 [256], P(('blk', 'rep')), may hold values from 1 to 2, as said below
- factor: bfloat16 [8192, 256], P('blk', 'rep'), may hold values from -0.19743253 to 0.19743253
Outputs:
- gradient: float32 [8192, 256], P('blk', 'rep')
Inputs may be any that keep to these rules, and one draw needn't show every extreme that they name: `triples`: each row is i >= j >= k; equal indices occur; the different row blocks named by the 2 slots of one device have different values of block // 2. `slot_count`: the first device's entry is 2.
All inputs are finite; a program needn't handle non-finite values.
Results may differ from a plain program's by a relative error of at most 0.003.
Values may be sent and summed in bfloat16 or wider, within the bound.
No kernel may reach another device: no remote copies, remote signals or barrier semaphores. Data moves between devices by JAX's collectives and lax.ppermute only.
A program may use at most 128 MiB of HBM per device.

v0:
```python
import jax
import jax.numpy as jnp
from jax import lax
from jax.experimental import pallas as pl
from jax.experimental.pallas import tpu as pltpu
from jax.sharding import Mesh
from jax.sharding import PartitionSpec as P


BLK = ("blk_0", "blk_1")
BLK_REP = ("blk_0", "blk_1", "rep")

BS = 128
CHUNK = 8
SUBLANES = 8
F32 = jnp.float32
BF16 = jnp.bfloat16
F16 = jnp.float16
VMEM = pltpu.VMEM
SMEM = pltpu.SMEM


def whole(space=VMEM):
    return pl.BlockSpec(memory_space=space)


def near(array):
    return pltpu.with_memory_space_constraint(array, VMEM)


def select_kernel(names, place, table, out):
    reps, named = names.shape
    for peer in range(reps):
        back = lax.rem(place[0] + reps - peer, reps)
        for t in range(named):
            out[peer, t] = table[names[back, t]]


def gram_kernel(rows, gram):
    reps, per_owner, width, _ = rows.shape
    total = jnp.zeros(gram.shape, F32)
    for t in range(per_owner):
        total = total + lax.dot_general(
            rows[0, t],
            rows[:, t].reshape(reps * width, BS),
            (((1,), (1,)), ((), ())),
            preferred_element_type=F32,
        )
    gram[...] = total


def fit_kernel(grams, rows, fitted):
    reps, per_owner, width, _ = rows.shape
    gram = grams[0]
    for source in range(1, grams.shape[0]):
        gram = gram + grams[source]
    rest = gram * gram
    pieces = []
    for _ in range(3):
        piece = rest.astype(BF16)
        rest = rest - piece.astype(F32)
        pieces.append(piece)
    for t in range(per_owner):
        block = rows[:, t].reshape(reps * width, BS)
        value = jnp.dot(pieces[2], block, preferred_element_type=F32)
        value = value + jnp.dot(pieces[1], block, preferred_element_type=F32)
        fitted[t] = value + jnp.dot(pieces[0], block, preferred_element_type=F32)


def fetch(source, target, arrived, piece):
    held = 2 * CHUNK
    per_slot = BS // held
    slot = piece // per_slot
    rows = pl.ds((piece - slot * per_slot) * held, held)
    return pltpu.make_async_copy(source.at[slot, rows], target.at[slot, rows], arrived.at[piece])


def contract_kernel(
    triples, count, x_far, sel, out,
    x, arrived, fac, low, mid, lower_a, middle_a, lower_b, middle_b, y1, y2, y3,
):
    slots = x.shape[0]
    reps, _, width, _ = sel.shape
    rank = reps * width
    per_slot = BS // CHUNK
    chunks = slots * per_slot
    pieces = chunks // 2
    for piece in range(pieces):
        fetch(x_far, x, arrived, piece).start()
    for slot in range(slots):
        for side in range(3):
            turned = sel[:, slot * 3 + side].reshape(rank, BS).astype(F32).T
            if side < 2:
                fac[slot, side] = turned
            if side == 2:
                low[slot] = turned.astype(BF16)
            if side == 1:
                mid[slot] = turned.astype(BF16)
    y2[...] = jnp.zeros_like(y2)
    y3[...] = jnp.zeros_like(y3)

    def multiply(chunk, lower_s, middle_s):
        slot = chunk // per_slot
        row0 = pl.multiple_of(lax.rem(chunk, per_slot) * CHUNK, CHUNK)
        blocks = x[slot, pl.ds(row0, CHUNK)]
        lower_s[...] = jnp.dot(
            blocks.reshape(CHUNK * BS, BS), low[slot], preferred_element_type=F32
        ).reshape(CHUNK, BS, rank)
        turned = jnp.concatenate([blocks[a].T for a in range(CHUNK)], axis=0)
        middle_s[...] = jnp.dot(turned, mid[slot], preferred_element_type=F32).reshape(
            CHUNK, BS, rank
        )

    def reduce(chunk, lower_s, middle_s):
        slot = chunk // per_slot
        row0 = pl.multiple_of(lax.rem(chunk, per_slot) * CHUNK, CHUNK)
        for half in range(rank // BS):
            cols = slice(half * BS, (half + 1) * BS)
            upper_rows = fac[slot, 0, pl.ds(row0, CHUNK), cols]
            spread = [
                jnp.broadcast_to(upper_rows[a : a + 1], (SUBLANES, BS)) for a in range(CHUNK)
            ]
            sums = [jnp.zeros((SUBLANES, BS), F32) for _ in range(CHUNK)]
            for b in range(0, BS, SUBLANES):
                rows = slice(b, b + SUBLANES)
                other = fac[slot, 1, rows, cols]
                second = y2[slot, rows, cols]
                third = y3[slot, rows, cols]
                for a in range(CHUNK):
                    value = lower_s[a, rows, cols]
                    sums[a] = sums[a] + value * other
                    second = second + value * spread[a]
                    third = third + middle_s[a, rows, cols] * spread[a]
                y2[slot, rows, cols] = second
                y3[slot, rows, cols] = third
            y1[slot, pl.ds(row0, CHUNK), cols] = jnp.concatenate(
                [jnp.sum(sums[a], axis=0, keepdims=True) for a in range(CHUNK)], axis=0
            )

    fetch(x_far, x, arrived, 0).wait()
    multiply(0, lower_a, middle_a)

    def pair(step, carry):
        @pl.when(step + 1 < pieces)
        def _():
            fetch(x_far, x, arrived, step + 1).wait()

        multiply(2 * step + 1, lower_b, middle_b)
        reduce(2 * step, lower_a, middle_a)
        multiply(jnp.minimum(2 * step + 2, chunks - 1), lower_a, middle_a)
        reduce(2 * step + 1, lower_b, middle_b)
        return carry

    lax.fori_loop(0, chunks // 2, pair, 0)

    for slot in range(slots):
        i, j, k = triples[slot, 0], triples[slot, 1], triples[slot, 2]
        upper_tie = i == j
        lower_tie = j == k
        alive = jnp.where(slot < count[0], 1.0, 0.0)
        base = jnp.where(upper_tie | lower_tie, 1.0, 2.0) * alive
        dropped = jnp.where(upper_tie & lower_tie, 0.0, base)
        for side, (value, weight) in enumerate(((y1, base), (y2, dropped), (y3, dropped))):
            out[:, slot * 3 + side] = (value[slot].T * weight).reshape(reps, width, BS)


def scatter_kernel(names, place, parts, out, total):
    reps, named = names.shape
    owners = out.shape[0]
    width = parts.shape[2]
    per_owner = total.shape[0] // owners
    total[...] = jnp.zeros_like(total)
    for peer in range(reps):
        back = lax.rem(place[0] + reps - peer, reps)
        for t in range(named):
            at = names[back, t]
            total[at] = total[at] + parts[peer, t]
    top = jnp.max(jnp.abs(total[...]), axis=(0, 1), keepdims=True)[0]
    top = jnp.max(top, axis=1, keepdims=True)
    power = jnp.clip(14.0 - jnp.ceil(jnp.log2(jnp.maximum(top, 1e-36))), -100.0, 100.0)
    power = jnp.broadcast_to(power, (SUBLANES, BS))
    scale = jnp.exp2(power)
    scale = jnp.concatenate([scale] * (width // SUBLANES), axis=0)
    for owner in range(owners):
        for t in range(per_owner):
            out[owner, t * width : (t + 1) * width] = total[owner * per_owner + t] * scale
        out[owner, per_owner * width :] = power


def moved(array, axis, shift):
    peers = lax.axis_size(axis)
    return lax.ppermute(array, axis, [(i, (i + shift) % peers) for i in range(peers)])


def from_each(array, axis):
    peers = lax.axis_size(axis)
    return jnp.stack([array] + [moved(array, axis, shift) for shift in range(1, peers)])


def shards(tensor_blocks, triples, slot_count, factor):
    slots = tensor_blocks.shape[0]
    reps = lax.axis_size("rep")
    owners = lax.axis_size(BLK)
    rows, width = factor.shape
    per_owner = rows // BS
    rank = reps * width
    named = 3 * slots
    place = lax.axis_index("rep").astype(jnp.int32).reshape(1)
    own = factor.T.reshape(width, per_owner, BS).swapaxes(0, 1)

    table = lax.all_to_all(
        jnp.broadcast_to(own[None], (owners, *own.shape)), BLK, 0, 0, tiled=True
    ).reshape(owners * per_owner, width, BS)

    listed = jnp.pad(triples.reshape(1, named).astype(BF16), ((0, 15), (0, BS - named)))
    around = from_each(jnp.concatenate([own.reshape(per_owner * width, BS), listed]), "rep")
    names = around[:, per_owner * width, :named].astype(jnp.int32)
    own_rows = around[:, : per_owner * width].reshape(reps, per_owner, width, BS)
    gram = pl.pallas_call(
        gram_kernel,
        out_shape=jax.ShapeDtypeStruct((width, rank), F32),
        in_specs=[whole()],
        out_specs=whole(),
        compiler_params=pltpu.CompilerParams(vmem_limit_bytes=16 << 20),
        name="gram",
    )(own_rows)

    chosen = pl.pallas_call(
        select_kernel,
        out_shape=VMEM((reps, named, width, BS), BF16),
        in_specs=[whole(SMEM), whole(SMEM), whole()],
        out_specs=whole(),
        compiler_params=pltpu.CompilerParams(vmem_limit_bytes=16 << 20),
        name="select",
    )(names, place, near(table))
    chosen = lax.all_to_all(chosen, "rep", 0, 0, tiled=True)

    gram = from_each(gram, "blk_1").sum(0)

    parts = pl.pallas_call(
        contract_kernel,
        out_shape=VMEM((reps, named, width, BS), F32),
        in_specs=[whole(SMEM), whole(SMEM), whole(pltpu.HBM), whole()],
        out_specs=whole(),
        scratch_shapes=[
            VMEM((slots, BS, BS, BS), BF16),
            pltpu.SemaphoreType.DMA((slots * BS // (2 * CHUNK),)),
            VMEM((slots, 2, BS, rank), F32),
            VMEM((slots, BS, rank), BF16),
            VMEM((slots, BS, rank), BF16),
            VMEM((CHUNK, BS, rank), F32),
            VMEM((CHUNK, BS, rank), F32),
            VMEM((CHUNK, BS, rank), F32),
            VMEM((CHUNK, BS, rank), F32),
            VMEM((slots, BS, rank), F32),
            VMEM((slots, BS, rank), F32),
            VMEM((slots, BS, rank), F32),
        ],
        compiler_params=pltpu.CompilerParams(vmem_limit_bytes=32 << 20),
        name="contract",
    )(
        triples,
        slot_count,
        pltpu.with_memory_space_constraint(tensor_blocks, pltpu.HBM),
        near(chosen),
    )
    parts = lax.all_to_all(parts, "rep", 0, 0, tiled=True)

    grams = from_each(gram, "blk_0")
    fitted = pl.pallas_call(
        fit_kernel,
        out_shape=jax.ShapeDtypeStruct((per_owner, width, BS), F32),
        in_specs=[whole(), whole()],
        out_specs=whole(),
        compiler_params=pltpu.CompilerParams(vmem_limit_bytes=16 << 20),
        name="fit",
    )(grams, own_rows)

    held = per_owner * width
    scaled = pl.pallas_call(
        scatter_kernel,
        out_shape=VMEM((owners, held + SUBLANES, BS), F32),
        in_specs=[whole(SMEM), whole(SMEM), whole()],
        out_specs=whole(),
        scratch_shapes=[VMEM((owners * per_owner, width, BS), F32)],
        compiler_params=pltpu.CompilerParams(vmem_limit_bytes=16 << 20),
        name="scatter",
    )(names, place, near(parts))
    arrived = lax.all_to_all(scaled.astype(F16), BLK, 0, 0, tiled=True)
    arrived = arrived.astype(F32)
    moment = (arrived[:, :held] * jnp.exp2(-arrived[:, held:, :1][:, :1])).sum(0)
    gradient = fitted - moment.reshape(per_owner, width, BS)
    return gradient.swapaxes(0, 1).reshape(width, rows).T


def solution(mesh):
    split = Mesh(mesh.devices.reshape(8, 4, mesh.shape["rep"]), ("blk_0", "blk_1", "rep"))
    in_specs = (P(BLK_REP, None, None, None), P(BLK_REP, None), P(BLK_REP), P(BLK, "rep"))
    out_specs = P(BLK, "rep")
    return jax.shard_map(
        shards, mesh=split, in_specs=in_specs, out_specs=out_specs, check_vma=False
    )
```

profile of v0, /device:TPU:8, one launch (start us, length us, event | category | flops | bytes accessed | tf_op | source)
XLA Modules:
  0.0 118.3 jit_solution(16112333021686595039)
XLA Ops:
  0.0 0.0 copy-start
  0.0 0.7 convert_element_type.27
  0.7 0.1 convert_element_type.28
  0.8 0.0 copy-done
  0.8 2.8 %collective-permute-start.5 = (bf16[80,128]{1,0:T(8,128)(2,1)S(1)}, bf16[80,128]{1,0:T(8,128)(2,1)S(1)}, u32[]{:S(2)}, u32[]{:S(2)}) collective-permute-start(bf16[80,128]{1,0:T(8,128)(2,1)S(1)} %fusion.2), channel_id=1, source_target_pairs={{0,6},{1,7},{2,0},{3,1},{4,2},{5,3},{6,4},{7,5},{8,14},{9,15},{10,... | collective-permute-start | bytes 61448 | tf_op jit(solution)/shard_map/ppermute | solution.py:192
  3.6 0.0 collective-permute-start.4
  3.6 2.7 %collective-permute-start.3 = (bf16[80,128]{1,0:T(8,128)(2,1)S(1)}, bf16[80,128]{1,0:T(8,128)(2,1)S(1)}, u32[]{:S(2)}, u32[]{:S(2)}) collective-permute-start(bf16[80,128]{1,0:T(8,128)(2,1)S(1)} %fusion.2), channel_id=1, source_target_pairs={{0,4},{1,5},{2,6},{3,7},{4,0},{5,1},{6,2},{7,3},{8,12},{9,13},{10,... | collective-permute-start | bytes 61448 | tf_op jit(solution)/shard_map/ppermute | solution.py:192
  6.3 0.0 collective-permute-start.2
  6.3 1.0 collective-permute-start
  7.3 0.9 broadcast_in_dim.2
  8.2 11.7 %all-to-all-start = ((bf16[32,2,32,128]{3,2,1,0:T(8,128)(2,1)}), bf16[32,2,32,128]{3,2,1,0:T(8,128)(2,1)S(1)}, u32[]{:S(2)}, u32[]{:S(2)}) async-start(bf16[32,2,32,128]{3,2,1,0:T(8,128)(2,1)} %broadcast_in_dim.2), calls=%async_computation | async-start | bytes 1048576 | tf_op jit(solution)/shard_map/all_to_all | solution.py:211
  19.9 0.0 copy-start.1
  20.0 0.0 collective-permute-done
  20.0 0.9 collective-permute-start.1
  20.9 4.1 %collective-permute-done.1 = bf16[80,128]{1,0:T(8,128)(2,1)S(1)} collective-permute-done((bf16[80,128]{1,0:T(8,128)(2,1)S(1)}, bf16[80,128]{1,0:T(8,128)(2,1)S(1)}, u32[]{:S(2)}, u32[]{:S(2)}) %collective-permute-start.1) | collective-permute-done | bytes 20512 | tf_op jit(solution)/shard_map/ppermute | solution.py:192
  25.0 0.0 collective-permute-start.6
  25.0 0.0 collective-permute-done.2
  25.1 0.0 collective-permute-done.3
  25.1 0.0 collective-permute-done.4
  25.1 0.0 collective-permute-done.5
  25.1 1.4 %collective-permute-done.6 = bf16[80,128]{1,0:T(8,128)(2,1)S(1)} collective-permute-done((bf16[80,128]{1,0:T(8,128)(2,1)S(1)}, bf16[80,128]{1,0:T(8,128)(2,1)S(1)}, u32[]{:S(2)}, u32[]{:S(2)}) %collective-permute-start.6) | collective-permute-done | bytes 20512 | tf_op jit(solution)/shard_map/ppermute | solution.py:192
  26.5 10.6 %all-to-all-done = bf16[32,2,32,128]{3,2,1,0:T(8,128)(2,1)S(1)} async-done(((bf16[32,2,32,128]{3,2,1,0:T(8,128)(2,1)}), bf16[32,2,32,128]{3,2,1,0:T(8,128)(2,1)S(1)}, u32[]{:S(2)}, u32[]{:S(2)}) %all-to-all-start) | async-done | bytes 524320 | tf_op jit(solution)/shard_map/all_to_all | solution.py:211
  37.1 1.4 %select.8 = bf16[8,6,32,128]{3,2,1,0:T(8,128)(2,1)} custom-call(s32[8,6]{1,0:T(8,128)S(1)} %bitcast.60, s32[1]{0:T(128)} %bitcast.21.place, bf16[64,32,128]{2,1,0:T(8,128)(2,1)S(1)} %bitcast.57), custom_call_target="tpu_custom_call" | custom-call | tf_op jit(solution)/shard_map/select/pallas_call | solution.py:228
  38.6 3.7 %all-to-all-start.1 = ((bf16[8,6,32,128]{3,2,1,0:T(8,128)(2,1)}), bf16[8,6,32,128]{3,2,1,0:T(8,128)(2,1)S(1)}, u32[]{:S(2)}, u32[]{:S(2)}) async-start(bf16[8,6,32,128]{3,2,1,0:T(8,128)(2,1)} %select.8), calls=%async_computation.1 | async-start | bytes 786432 | tf_op jit(solution)/shard_map/all_to_all | solution.py:236
  43.0 8.3 %all-to-all-done.1.sel = bf16[8,6,32,128]{3,2,1,0:T(8,128)(2,1)S(1)} async-done(((bf16[8,6,32,128]{3,2,1,0:T(8,128)(2,1)}), bf16[8,6,32,128]{3,2,1,0:T(8,128)(2,1)S(1)}, u32[]{:S(2)}, u32[]{:S(2)}) %all-to-all-start.1) | async-done | bytes 393248 | tf_op jit(solution)/shard_map/all_to_all | solution.py:236
  51.2 0.0 copy-done.1
  51.2 16.7 %contract.1 = f32[8,6,32,128]{3,2,1,0:T(8,128)} custom-call(s32[2,3]{1,0:T(2,128)S(1)} %copy-done.1, s32[1]{0:T(128)S(6)} %copy.36.count, bf16[2,128,128,128]{3,2,1,0:T(8,128)(2,1)} %x_far.1, bf16[8,6,32,128]{3,2,1,0:T(8,128)(2,1)S(1)} %all-to-all-done.1.sel), custom_call_target="tpu_custom_call" | custom-call | tf_op jit(solution)/shard_map/contract/pallas_call | solution.py:240
  67.9 3.6 %all-to-all-start.2 = ((f32[8,6,32,128]{3,2,1,0:T(8,128)}), f32[8,6,32,128]{3,2,1,0:T(8,128)S(1)}, u32[]{:S(2)}, u32[]{:S(2)}) async-start(f32[8,6,32,128]{3,2,1,0:T(8,128)} %contract.1), calls=%async_computation.2 | async-start | bytes 1572864 | tf_op jit(solution)/shard_map/all_to_all | solution.py:267
  71.5 0.1 gram.1
  71.6 1.2 %collective-permute-start.9 = (f32[32,256]{1,0:T(8,128)S(1)}, f32[32,256]{1,0:T(8,128)S(1)}, u32[]{:S(2)}, u32[]{:S(2)}) collective-permute-start(f32[32,256]{1,0:T(8,128)S(1)} %gram.1), channel_id=1, source_target_pairs={{0,24},{8,0},{16,8},{24,16},{1,25},{9,1},{17,9},{25,17},{2,26},{10... | collective-permute-start | bytes 98312 | tf_op jit(solution)/shard_map/ppermute | solution.py:192
  72.9 1.7 %collective-permute-start.8 = (f32[32,256]{1,0:T(8,128)S(1)}, f32[32,256]{1,0:T(8,128)S(1)}, u32[]{:S(2)}, u32[]{:S(2)}) collective-permute-start(f32[32,256]{1,0:T(8,128)S(1)} %gram.1), channel_id=1, source_target_pairs={{0,16},{8,24},{16,0},{24,8},{1,17},{9,25},{17,1},{25,9},{2,18},{10... | collective-permute-start | bytes 98312 | tf_op jit(solution)/shard_map/ppermute | solution.py:192
  74.6 1.8 %collective-permute-start.7 = (f32[32,256]{1,0:T(8,128)S(1)}, f32[32,256]{1,0:T(8,128)S(1)}, u32[]{:S(2)}, u32[]{:S(2)}) collective-permute-start(f32[32,256]{1,0:T(8,128)S(1)} %gram.1), channel_id=1, source_target_pairs={{0,8},{8,16},{16,24},{24,0},{1,9},{9,17},{17,25},{25,1},{2,10},{10... | collective-permute-start | bytes 98312 | tf_op jit(solution)/shard_map/ppermute | solution.py:192
  76.4 0.0 collective-permute-done.9
  76.4 1.9 %collective-permute-done.8 = f32[32,256]{1,0:T(8,128)S(1)} collective-permute-done((f32[32,256]{1,0:T(8,128)S(1)}, f32[32,256]{1,0:T(8,128)S(1)}, u32[]{:S(2)}, u32[]{:S(2)}) %collective-permute-start.8) | collective-permute-done | bytes 32800 | tf_op jit(solution)/shard_map/ppermute | solution.py:192
  78.3 0.2 collective-permute-done.7
  78.5 1.1 collective-permute-start.10
  79.6 0.7 collective-permute-start.15
  80.3 3.1 %collective-permute-start.14 = (f32[32,256]{1,0:T(8,128)S(1)}, f32[32,256]{1,0:T(8,128)S(1)}, u32[]{:S(2)}, u32[]{:S(2)}) collective-permute-start(f32[32,256]{1,0:T(8,128)S(1)} %get-tuple-element.6), channel_id=1, source_target_pairs={{0,160},{32,192},{64,224},{96,0},{128,32},{160,64},{192,96},{224,1... | collective-permute-start | bytes 98312 | tf_op jit(solution)/shard_map/ppermute | solution.py:192
  83.4 4.4 %collective-permute-start.13 = (f32[32,256]{1,0:T(8,128)S(1)}, f32[32,256]{1,0:T(8,128)S(1)}, u32[]{:S(2)}, u32[]{:S(2)}) collective-permute-start(f32[32,256]{1,0:T(8,128)S(1)} %get-tuple-element.6), channel_id=1, source_target_pairs={{0,128},{32,160},{64,192},{96,224},{128,0},{160,32},{192,64},{224,... | collective-permute-start | bytes 98312 | tf_op jit(solution)/shard_map/ppermute | solution.py:192
  87.8 0.5 collective-permute-start.12
  88.3 0.0 collective-permute-done.10
  88.3 1.0 collective-permute-start.11
  89.3 0.0 all-to-all-done.2.parts
  89.3 1.1 scatter.1
  90.4 0.9 convert_element_type.31
  91.3 9.7 %all-to-all-start.3 = ((f16[32,72,128]{2,1,0:T(8,128)(2,1)}), f16[32,72,128]{2,1,0:T(8,128)(2,1)S(1)}, u32[]{:S(2)}, u32[]{:S(2)}) async-start(f16[32,72,128]{2,1,0:T(8,128)(2,1)} %convert_element_type.31), calls=%async_computation.3 | async-start | bytes 1179648 | tf_op jit(solution)/shard_map/all_to_all | solution.py:289
  101.0 0.0 collective-permute-done.11
  101.1 2.8 %collective-permute-start.16 = (f32[32,256]{1,0:T(8,128)S(1)}, f32[32,256]{1,0:T(8,128)S(1)}, u32[]{:S(2)}, u32[]{:S(2)}) collective-permute-start(f32[32,256]{1,0:T(8,128)S(1)} %get-tuple-element.6), channel_id=1, source_target_pairs={{0,224},{32,0},{64,32},{96,64},{128,96},{160,128},{192,160},{224,1... | collective-permute-start | bytes 98312 | tf_op jit(solution)/shard_map/ppermute | solution.py:192
  103.9 0.0 collective-permute-done.12
  103.9 0.0 collective-permute-done.13
  103.9 0.0 collective-permute-done.14
  103.9 0.0 collective-permute-done.15
  104.0 9.9 %collective-permute-done.16 = f32[32,256]{1,0:T(8,128)S(1)} collective-permute-done((f32[32,256]{1,0:T(8,128)S(1)}, f32[32,256]{1,0:T(8,128)S(1)}, u32[]{:S(2)}, u32[]{:S(2)}) %collective-permute-start.16) | collective-permute-done | bytes 32800 | tf_op jit(solution)/shard_map/ppermute | solution.py:192
  113.9 0.2 fit.1
  114.1 3.0 %all-to-all-done.3 = f16[32,72,128]{2,1,0:T(8,128)(2,1)S(1)} async-done(((f16[32,72,128]{2,1,0:T(8,128)(2,1)}), f16[32,72,128]{2,1,0:T(8,128)(2,1)S(1)}, u32[]{:S(2)}, u32[]{:S(2)}) %all-to-all-start.3) | async-done | bytes 589856 | tf_op jit(solution)/shard_map/all_to_all | solution.py:289
  117.1 0.1 convert_element_type.32
  117.2 0.3 fusion.5
  117.5 0.1 fusion
  117.6 0.6 bitcast_bitcast_fusion
  (20 shorter events, 0.1 us)
Async XLA Ops:
  0.0 0.8 copy-start
  0.8 24.3 %collective-permute-start.5 = (bf16[80,128]{1,0:T(8,128)(2,1)S(1)}, bf16[80,128]{1,0:T(8,128)(2,1)S(1)}, u32[]{:S(2)}, u32[]{:S(2)}) collective-permute-start(bf16[80,128]{1,0:T(8,128)(2,1)S(1)} %fusion.2), channel_id=1, source_target_pairs={{0,6},{1,7},{2,0},{3,1},{4,2},{5,3},{6,4},{7,5},{8,14},{9,15},{10,... | collective-permute-start | bytes 61448 | tf_op jit(solution)/shard_map/ppermute | solution.py:192
  3.6 21.5 %collective-permute-start.4 = (bf16[80,128]{1,0:T(8,128)(2,1)S(1)}, bf16[80,128]{1,0:T(8,128)(2,1)S(1)}, u32[]{:S(2)}, u32[]{:S(2)}) collective-permute-start(bf16[80,128]{1,0:T(8,128)(2,1)S(1)} %fusion.2), channel_id=1, source_target_pairs={{0,5},{1,6},{2,7},{3,0},{4,1},{5,2},{6,3},{7,4},{8,13},{9,14},{10,... | collective-permute-start | bytes 61448 | tf_op jit(solution)/shard_map/ppermute | solution.py:192
  3.6 21.4 %collective-permute-start.3 = (bf16[80,128]{1,0:T(8,128)(2,1)S(1)}, bf16[80,128]{1,0:T(8,128)(2,1)S(1)}, u32[]{:S(2)}, u32[]{:S(2)}) collective-permute-start(bf16[80,128]{1,0:T(8,128)(2,1)S(1)} %fusion.2), channel_id=1, source_target_pairs={{0,4},{1,5},{2,6},{3,7},{4,0},{5,1},{6,2},{7,3},{8,12},{9,13},{10,... | collective-permute-start | bytes 61448 | tf_op jit(solution)/shard_map/ppermute | solution.py:192
  6.3 18.7 %collective-permute-start.2 = (bf16[80,128]{1,0:T(8,128)(2,1)S(1)}, bf16[80,128]{1,0:T(8,128)(2,1)S(1)}, u32[]{:S(2)}, u32[]{:S(2)}) collective-permute-start(bf16[80,128]{1,0:T(8,128)(2,1)S(1)} %fusion.2), channel_id=1, source_target_pairs={{0,3},{1,4},{2,5},{3,6},{4,7},{5,0},{6,1},{7,2},{8,11},{9,12},{10,... | collective-permute-start | bytes 61448 | tf_op jit(solution)/shard_map/ppermute | solution.py:192
  6.3 13.6 %collective-permute-start = (bf16[80,128]{1,0:T(8,128)(2,1)S(1)}, bf16[80,128]{1,0:T(8,128)(2,1)S(1)}, u32[]{:S(2)}, u32[]{:S(2)}) collective-permute-start(bf16[80,128]{1,0:T(8,128)(2,1)S(1)} %fusion.2), channel_id=1, source_target_pairs={{0,1},{1,2},{2,3},{3,4},{4,5},{5,6},{6,7},{7,0},{8,9},{9,10},{10,1... | collective-permute-start | bytes 61448 | tf_op jit(solution)/shard_map/ppermute | solution.py:192
  8.2 28.9 %all-to-all-start = ((bf16[32,2,32,128]{3,2,1,0:T(8,128)(2,1)}), bf16[32,2,32,128]{3,2,1,0:T(8,128)(2,1)S(1)}, u32[]{:S(2)}, u32[]{:S(2)}) async-start(bf16[32,2,32,128]{3,2,1,0:T(8,128)(2,1)} %broadcast_in_dim.2), calls=%async_computation | async-start | bytes 1048576 | tf_op jit(solution)/shard_map/all_to_all | solution.py:211
  19.9 31.3 %copy-start.1 = (s32[2,3]{1,0:T(2,128)S(1)}, s32[2,3]{1,0:T(2,128)}, u32[]{:S(2)}) copy-start(s32[2,3]{1,0:T(2,128)} %triples.1) | copy-start | bytes 76
  20.0 5.1 %collective-permute-start.1 = (bf16[80,128]{1,0:T(8,128)(2,1)S(1)}, bf16[80,128]{1,0:T(8,128)(2,1)S(1)}, u32[]{:S(2)}, u32[]{:S(2)}) collective-permute-start(bf16[80,128]{1,0:T(8,128)(2,1)S(1)} %fusion.2), channel_id=1, source_target_pairs={{0,2},{1,3},{2,4},{3,5},{4,6},{5,7},{6,0},{7,1},{8,10},{9,11},{10,... | collective-permute-start | bytes 61448 | tf_op jit(solution)/shard_map/ppermute | solution.py:192
  25.0 1.5 %collective-permute-start.6 = (bf16[80,128]{1,0:T(8,128)(2,1)S(1)}, bf16[80,128]{1,0:T(8,128)(2,1)S(1)}, u32[]{:S(2)}, u32[]{:S(2)}) collective-permute-start(bf16[80,128]{1,0:T(8,128)(2,1)S(1)} %fusion.2), channel_id=1, source_target_pairs={{0,7},{1,0},{2,1},{3,2},{4,3},{5,4},{6,5},{7,6},{8,15},{9,8},{10,9... | collective-permute-start | bytes 61448 | tf_op jit(solution)/shard_map/ppermute | solution.py:192
  38.6 12.7 %all-to-all-start.1 = ((bf16[8,6,32,128]{3,2,1,0:T(8,128)(2,1)}), bf16[8,6,32,128]{3,2,1,0:T(8,128)(2,1)S(1)}, u32[]{:S(2)}, u32[]{:S(2)}) async-start(bf16[8,6,32,128]{3,2,1,0:T(8,128)(2,1)} %select.8), calls=%async_computation.1 | async-start | bytes 786432 | tf_op jit(solution)/shard_map/all_to_all | solution.py:236
  67.9 21.3 %all-to-all-start.2 = ((f32[8,6,32,128]{3,2,1,0:T(8,128)}), f32[8,6,32,128]{3,2,1,0:T(8,128)S(1)}, u32[]{:S(2)}, u32[]{:S(2)}) async-start(f32[8,6,32,128]{3,2,1,0:T(8,128)} %contract.1), calls=%async_computation.2 | async-start | bytes 1572864 | tf_op jit(solution)/shard_map/all_to_all | solution.py:267
  71.6 4.7 %collective-permute-start.9 = (f32[32,256]{1,0:T(8,128)S(1)}, f32[32,256]{1,0:T(8,128)S(1)}, u32[]{:S(2)}, u32[]{:S(2)}) collective-permute-start(f32[32,256]{1,0:T(8,128)S(1)} %gram.1), channel_id=1, source_target_pairs={{0,24},{8,0},{16,8},{24,16},{1,25},{9,1},{17,9},{25,17},{2,26},{10... | collective-permute-start | bytes 98312 | tf_op jit(solution)/shard_map/ppermute | solution.py:192
  72.9 5.4 %collective-permute-start.8 = (f32[32,256]{1,0:T(8,128)S(1)}, f32[32,256]{1,0:T(8,128)S(1)}, u32[]{:S(2)}, u32[]{:S(2)}) collective-permute-start(f32[32,256]{1,0:T(8,128)S(1)} %gram.1), channel_id=1, source_target_pairs={{0,16},{8,24},{16,0},{24,8},{1,17},{9,25},{17,1},{25,9},{2,18},{10... | collective-permute-start | bytes 98312 | tf_op jit(solution)/shard_map/ppermute | solution.py:192
  74.6 3.9 %collective-permute-start.7 = (f32[32,256]{1,0:T(8,128)S(1)}, f32[32,256]{1,0:T(8,128)S(1)}, u32[]{:S(2)}, u32[]{:S(2)}) collective-permute-start(f32[32,256]{1,0:T(8,128)S(1)} %gram.1), channel_id=1, source_target_pairs={{0,8},{8,16},{16,24},{24,0},{1,9},{9,17},{17,25},{25,1},{2,10},{10... | collective-permute-start | bytes 98312 | tf_op jit(solution)/shard_map/ppermute | solution.py:192
  78.5 9.7 %collective-permute-start.10 = (f32[32,256]{1,0:T(8,128)S(1)}, f32[32,256]{1,0:T(8,128)S(1)}, u32[]{:S(2)}, u32[]{:S(2)}) collective-permute-start(f32[32,256]{1,0:T(8,128)S(1)} %get-tuple-element.6), channel_id=1, source_target_pairs={{0,32},{32,64},{64,96},{96,128},{128,160},{160,192},{192,224},{224... | collective-permute-start | bytes 98312 | tf_op jit(solution)/shard_map/ppermute | solution.py:192
  79.6 24.4 %collective-permute-start.15 = (f32[32,256]{1,0:T(8,128)S(1)}, f32[32,256]{1,0:T(8,128)S(1)}, u32[]{:S(2)}, u32[]{:S(2)}) collective-permute-start(f32[32,256]{1,0:T(8,128)S(1)} %get-tuple-element.6), channel_id=1, source_target_pairs={{0,192},{32,224},{64,0},{96,32},{128,64},{160,96},{192,128},{224,1... | collective-permute-start | bytes 98312 | tf_op jit(solution)/shard_map/ppermute | solution.py:192
  80.3 23.6 %collective-permute-start.14 = (f32[32,256]{1,0:T(8,128)S(1)}, f32[32,256]{1,0:T(8,128)S(1)}, u32[]{:S(2)}, u32[]{:S(2)}) collective-permute-start(f32[32,256]{1,0:T(8,128)S(1)} %get-tuple-element.6), channel_id=1, source_target_pairs={{0,160},{32,192},{64,224},{96,0},{128,32},{160,64},{192,96},{224,1... | collective-permute-start | bytes 98312 | tf_op jit(solution)/shard_map/ppermute | solution.py:192
  83.4 20.5 %collective-permute-start.13 = (f32[32,256]{1,0:T(8,128)S(1)}, f32[32,256]{1,0:T(8,128)S(1)}, u32[]{:S(2)}, u32[]{:S(2)}) collective-permute-start(f32[32,256]{1,0:T(8,128)S(1)} %get-tuple-element.6), channel_id=1, source_target_pairs={{0,128},{32,160},{64,192},{96,224},{128,0},{160,32},{192,64},{224,... | collective-permute-start | bytes 98312 | tf_op jit(solution)/shard_map/ppermute | solution.py:192
  87.8 16.1 %collective-permute-start.12 = (f32[32,256]{1,0:T(8,128)S(1)}, f32[32,256]{1,0:T(8,128)S(1)}, u32[]{:S(2)}, u32[]{:S(2)}) collective-permute-start(f32[32,256]{1,0:T(8,128)S(1)} %get-tuple-element.6), channel_id=1, source_target_pairs={{0,96},{32,128},{64,160},{96,192},{128,224},{160,0},{192,32},{224,... | collective-permute-start | bytes 98312 | tf_op jit(solution)/shard_map/ppermute | solution.py:192
  88.3 12.8 %collective-permute-start.11 = (f32[32,256]{1,0:T(8,128)S(1)}, f32[32,256]{1,0:T(8,128)S(1)}, u32[]{:S(2)}, u32[]{:S(2)}) collective-permute-start(f32[32,256]{1,0:T(8,128)S(1)} %get-tuple-element.6), channel_id=1, source_target_pairs={{0,64},{32,96},{64,128},{96,160},{128,192},{160,224},{192,0},{224,... | collective-permute-start | bytes 98312 | tf_op jit(solution)/shard_map/ppermute | solution.py:192
  91.3 25.8 %all-to-all-start.3 = ((f16[32,72,128]{2,1,0:T(8,128)(2,1)}), f16[32,72,128]{2,1,0:T(8,128)(2,1)S(1)}, u32[]{:S(2)}, u32[]{:S(2)}) async-start(f16[32,72,128]{2,1,0:T(8,128)(2,1)} %convert_element_type.31), calls=%async_computation.3 | async-start | bytes 1179648 | tf_op jit(solution)/shard_map/all_to_all | solution.py:289
  101.1 12.8 %collective-permute-start.16 = (f32[32,256]{1,0:T(8,128)S(1)}, f32[32,256]{1,0:T(8,128)S(1)}, u32[]{:S(2)}, u32[]{:S(2)}) collective-permute-start(f32[32,256]{1,0:T(8,128)S(1)} %get-tuple-element.6), channel_id=1, source_target_pairs={{0,224},{32,0},{64,32},{96,64},{128,96},{160,128},{192,160},{224,1... | collective-permute-start | bytes 98312 | tf_op jit(solution)/shard_map/ppermute | solution.py:192
where the time goes:
time: 120 us; the launch traced here: 118 us
  starting transfers between devices  54.4 us (45%)
  waiting for transfers between devices  39.5 us (33%)
  Pallas kernels  19.5 us (16%)
  other arithmetic  2.81 us (2%)
    ppermute x17, starting transfers between devices, moved(): lax.ppermute(array, axis, [(i, (i + shift) % peers) for i in range(peers)])  25.7 us
    ppermute x17, waiting for transfers between devices, moved(): lax.ppermute(array, axis, [(i, (i + shift) % peers) for i in range(peers)])  17.6 us
    pallas_call x1, Pallas kernels, shards(): pl.pallas_call(contract_kernel, out_shape=VMEM((reps, named, width, BS),...  16.7 us
    all_to_all x1, starting transfers between devices, shards(): lax.all_to_all(jnp.broadcast_to(own[None], (owners, *own.shape)), BLK, 0,...  11.7 us
    all_to_all x1, waiting for transfers between devices, shards(): lax.all_to_all(jnp.broadcast_to(own[None], (owners, *own.shape)), BLK, 0,...  10.6 us
    all_to_all x1, starting transfers between devices, shards(): arrived = lax.all_to_all(scaled.astype(F16), BLK, 0, 0, tiled=True)  9.75 us
    all_to_all x1, waiting for transfers between devices, shards(): chosen = lax.all_to_all(chosen, 'rep', 0, 0, tiled=True)  8.26 us
    all_to_all x1, starting transfers between devices, shards(): chosen = lax.all_to_all(chosen, 'rep', 0, 0, tiled=True)  3.74 us
  transfers between devices with their start and end apart: 21, of which 8 were waited for; matrix products, arithmetic and copies ran while one was open for 2% of the time, Pallas kernels for 1%

commit v1 on v0

--- a/solution.py
+++ b/solution.py
@@ -13,6 +13,8 @@
 BS = 128
 CHUNK = 8
 SUBLANES = 8
+STEP = 4
+AHEAD = 3
 F32 = jnp.float32
 BF16 = jnp.bfloat16
 F16 = jnp.float16
@@ -49,12 +51,9 @@
     gram[...] = total
 
 
-def fit_kernel(grams, rows, fitted):
+def fit_kernel(gram, rows, fitted):
     reps, per_owner, width, _ = rows.shape
-    gram = grams[0]
-    for source in range(1, grams.shape[0]):
-        gram = gram + grams[source]
-    rest = gram * gram
+    rest = gram[...] * gram[...]
     pieces = []
     for _ in range(3):
         piece = rest.astype(BF16)
@@ -68,7 +67,7 @@
 
 
 def fetch(source, target, arrived, piece):
-    held = 2 * CHUNK
+    held = STEP * CHUNK
     per_slot = BS // held
     slot = piece // per_slot
     rows = pl.ds((piece - slot * per_slot) * held, held)
@@ -84,8 +83,8 @@
     rank = reps * width
     per_slot = BS // CHUNK
     chunks = slots * per_slot
-    pieces = chunks // 2
-    for piece in range(pieces):
+    pieces = chunks // STEP
+    for piece in range(min(AHEAD, pieces)):
         fetch(x_far, x, arrived, piece).start()
     for slot in range(slots):
         for side in range(3):
@@ -140,18 +139,25 @@
     fetch(x_far, x, arrived, 0).wait()
     multiply(0, lower_a, middle_a)
 
-    def pair(step, carry):
+    def several(step, carry):
+        @pl.when(step + AHEAD < pieces)
+        def _():
+            fetch(x_far, x, arrived, step + AHEAD).start()
+
         @pl.when(step + 1 < pieces)
         def _():
             fetch(x_far, x, arrived, step + 1).wait()
 
-        multiply(2 * step + 1, lower_b, middle_b)
-        reduce(2 * step, lower_a, middle_a)
-        multiply(jnp.minimum(2 * step + 2, chunks - 1), lower_a, middle_a)
-        reduce(2 * step + 1, lower_b, middle_b)
+        first = step * STEP
+        for n in range(STEP):
+            here, there = (lower_a, middle_a), (lower_b, middle_b)
+            if n % 2:
+                here, there = there, here
+            multiply(jnp.minimum(first + n + 1, chunks - 1), *there)
+            reduce(first + n, *here)
         return carry
 
-    lax.fori_loop(0, chunks // 2, pair, 0)
+    lax.fori_loop(0, pieces, several, 0)
 
     for slot in range(slots):
         i, j, k = triples[slot, 0], triples[slot, 1], triples[slot, 2]
@@ -197,6 +203,16 @@
     return jnp.stack([array] + [moved(array, axis, shift) for shift in range(1, peers)])
 
 
+def summed(array, axis):
+    peers = lax.axis_size(axis)
+    bit = 1
+    while bit < peers:
+        swap = [(i, i ^ bit) for i in range(peers)]
+        array = array + lax.ppermute(array, axis, swap)
+        bit *= 2
+    return array
+
+
 def shards(tensor_blocks, triples, slot_count, factor):
     slots = tensor_blocks.shape[0]
     reps = lax.axis_size("rep")
@@ -235,7 +251,7 @@
     )(names, place, near(table))
     chosen = lax.all_to_all(chosen, "rep", 0, 0, tiled=True)
 
-    gram = from_each(gram, "blk_1").sum(0)
+    gram = summed(gram, "blk_1")
 
     parts = pl.pallas_call(
         contract_kernel,
@@ -244,7 +260,7 @@
         out_specs=whole(),
         scratch_shapes=[
             VMEM((slots, BS, BS, BS), BF16),
-            pltpu.SemaphoreType.DMA((slots * BS // (2 * CHUNK),)),
+            pltpu.SemaphoreType.DMA((slots * BS // (STEP * CHUNK),)),
             VMEM((slots, 2, BS, rank), F32),
             VMEM((slots, BS, rank), BF16),
             VMEM((slots, BS, rank), BF16),
@@ -266,7 +282,7 @@
     )
     parts = lax.all_to_all(parts, "rep", 0, 0, tiled=True)
 
-    grams = from_each(gram, "blk_0")
+    gram = summed(gram, "blk_0")
     fitted = pl.pallas_call(
         fit_kernel,
         out_shape=jax.ShapeDtypeStruct((per_owner, width, BS), F32),
@@ -274,7 +290,7 @@
         out_specs=whole(),
         compiler_params=pltpu.CompilerParams(vmem_limit_bytes=16 << 20),
         name="fit",
-    )(grams, own_rows)
+    )(gram, own_rows)
 
     held = per_owner * width
     scaled = pl.pallas_call(

time: 120 us -> 118 us (0.983); the launches traced: 118 us -> 118 us
  blocking collectives: 0 us -> 15.6 us
  starting transfers between devices: 54.4 us -> 41.1 us
  Pallas kernels: 19.5 us -> 17.2 us
    ppermute x17 -> x7, starting transfers between devices: 25.7 us -> 7.41 us  [moved(): lax.ppermute(array, axis, [(i, (i + shift) % peers) for i in range(peers)])]
    all_to_all x0 -> x1, blocking collectives: none -> 15.6 us  [shards(): parts = lax.all_to_all(parts, 'rep', 0, 0, tiled=True)]
    ppermute x0 -> x5, waiting for transfers between devices: none -> 14.5 us  [summed(): array = array + lax.ppermute(array, axis, swap)]
    ppermute x0 -> x5, starting transfers between devices: none -> 12.7 us  [summed(): array = array + lax.ppermute(array, axis, swap)]
    ppermute x17 -> x7, waiting for transfers between devices: 17.6 us -> 5.53 us  [moved(): lax.ppermute(array, axis, [(i, (i + shift) % peers) for i in range(peers)])]
    all_to_all x1, starting transfers between devices: 9.75 us -> 5.57 us  [shards(): arrived = lax.all_to_all(scaled.astype(F16), BLK, 0, 0, tiled=True)]
    all_to_all x1 -> x0, starting transfers between devices: 3.56 us -> none  [shards(): parts = lax.all_to_all(parts, 'rep', 0, 0, tiled=True)]
    all_to_all x1, waiting for transfers between devices: 3.02 us -> 0.01 us  [shards(): arrived = lax.all_to_all(scaled.astype(F16), BLK, 0, 0, tiled=True)]
  transfers between devices with their start and end apart: 21 -> 15, of which waited for: 8 -> 9; matrix products, arithmetic and copies ran while one was open for 2% -> 1% of each run, Pallas kernels for 1% -> 0%
where the time goes in v1:
time: 118 us
  starting transfers between devices  41.1 us (35%)
  waiting for transfers between devices  38.9 us (33%)
  Pallas kernels  17.2 us (15%)
  blocking collectives  15.6 us (13%)
  other arithmetic  2.81 us (2%)
    all_to_all x1, blocking collectives, shards(): parts = lax.all_to_all(parts, 'rep', 0, 0, tiled=True)  15.6 us
    ppermute x5, waiting for transfers between devices, summed(): array = array + lax.ppermute(array, axis, swap)  14.5 us
    pallas_call x1, Pallas kernels, shards(): pl.pallas_call(contract_kernel, out_shape=VMEM((reps, named, width, BS),...  14.4 us
    ppermute x5, starting transfers between devices, summed(): array = array + lax.ppermute(array, axis, swap)  12.7 us
    all_to_all x1, starting transfers between devices, shards(): lax.all_to_all(jnp.broadcast_to(own[None], (owners, *own.shape)), BLK, 0,...  11.7 us
    all_to_all x1, waiting for transfers between devices, shards(): lax.all_to_all(jnp.broadcast_to(own[None], (owners, *own.shape)), BLK, 0,...  10.6 us
    all_to_all x1, waiting for transfers between devices, shards(): chosen = lax.all_to_all(chosen, 'rep', 0, 0, tiled=True)  8.26 us
    ppermute x7, starting transfers between devices, moved(): lax.ppermute(array, axis, [(i, (i + shift) % peers) for i in range(peers)])  7.41 us
  transfers between devices with their start and end apart: 15, of which 9 were waited for; matrix products, arithmetic and copies ran while one was open for 1% of the time, Pallas kernels for 0%

profile of v1, /device:TPU:8, one launch (start us, length us, event | category | flops | bytes accessed | tf_op | source)
XLA Modules:
  0.0 117.5 jit_solution(6478856674397619958)
XLA Ops:
  0.0 0.0 copy-start
  0.0 0.7 convert_element_type.27
  0.7 0.1 convert_element_type.28
  0.8 0.0 copy-done
  0.8 2.8 %collective-permute-start.5 = (bf16[80,128]{1,0:T(8,128)(2,1)S(1)}, bf16[80,128]{1,0:T(8,128)(2,1)S(1)}, u32[]{:S(2)}, u32[]{:S(2)}) collective-permute-start(bf16[80,128]{1,0:T(8,128)(2,1)S(1)} %fusion.2), channel_id=1, source_target_pairs={{0,6},{1,7},{2,0},{3,1},{4,2},{5,3},{6,4},{7,5},{8,14},{9,15},{10,... | collective-permute-start | bytes 61448 | tf_op jit(solution)/shard_map/ppermute | solution.py:198
  3.6 0.0 collective-permute-start.4
  3.6 2.7 %collective-permute-start.3 = (bf16[80,128]{1,0:T(8,128)(2,1)S(1)}, bf16[80,128]{1,0:T(8,128)(2,1)S(1)}, u32[]{:S(2)}, u32[]{:S(2)}) collective-permute-start(bf16[80,128]{1,0:T(8,128)(2,1)S(1)} %fusion.2), channel_id=1, source_target_pairs={{0,4},{1,5},{2,6},{3,7},{4,0},{5,1},{6,2},{7,3},{8,12},{9,13},{10,... | collective-permute-start | bytes 61448 | tf_op jit(solution)/shard_map/ppermute | solution.py:198
  6.3 0.0 collective-permute-start.2
  6.3 1.0 collective-permute-start
  7.3 0.9 broadcast_in_dim.2
  8.2 11.7 %all-to-all-start = ((bf16[32,2,32,128]{3,2,1,0:T(8,128)(2,1)}), bf16[32,2,32,128]{3,2,1,0:T(8,128)(2,1)S(1)}, u32[]{:S(2)}, u32[]{:S(2)}) async-start(bf16[32,2,32,128]{3,2,1,0:T(8,128)(2,1)} %broadcast_in_dim.2), calls=%async_computation | async-start | bytes 1048576 | tf_op jit(solution)/shard_map/all_to_all | solution.py:227
  19.9 0.0 copy-start.1
  19.9 0.0 collective-permute-done
  20.0 0.9 collective-permute-start.1
  20.9 4.1 %collective-permute-done.1 = bf16[80,128]{1,0:T(8,128)(2,1)S(1)} collective-permute-done((bf16[80,128]{1,0:T(8,128)(2,1)S(1)}, bf16[80,128]{1,0:T(8,128)(2,1)S(1)}, u32[]{:S(2)}, u32[]{:S(2)}) %collective-permute-start.1) | collective-permute-done | bytes 20512 | tf_op jit(solution)/shard_map/ppermute | solution.py:198
  25.0 0.0 collective-permute-start.6
  25.0 0.0 collective-permute-done.2
  25.1 0.0 collective-permute-done.3
  25.1 0.0 collective-permute-done.4
  25.1 0.0 collective-permute-done.5
  25.1 1.4 %collective-permute-done.6 = bf16[80,128]{1,0:T(8,128)(2,1)S(1)} collective-permute-done((bf16[80,128]{1,0:T(8,128)(2,1)S(1)}, bf16[80,128]{1,0:T(8,128)(2,1)S(1)}, u32[]{:S(2)}, u32[]{:S(2)}) %collective-permute-start.6) | collective-permute-done | bytes 20512 | tf_op jit(solution)/shard_map/ppermute | solution.py:198
  26.5 10.6 %all-to-all-done = bf16[32,2,32,128]{3,2,1,0:T(8,128)(2,1)S(1)} async-done(((bf16[32,2,32,128]{3,2,1,0:T(8,128)(2,1)}), bf16[32,2,32,128]{3,2,1,0:T(8,128)(2,1)S(1)}, u32[]{:S(2)}, u32[]{:S(2)}) %all-to-all-start) | async-done | bytes 524320 | tf_op jit(solution)/shard_map/all_to_all | solution.py:227
  37.1 1.4 %select.8 = bf16[8,6,32,128]{3,2,1,0:T(8,128)(2,1)} custom-call(s32[8,6]{1,0:T(8,128)S(1)} %bitcast.44, s32[1]{0:T(128)} %bitcast.13.place, bf16[64,32,128]{2,1,0:T(8,128)(2,1)S(1)} %bitcast.41), custom_call_target="tpu_custom_call" | custom-call | tf_op jit(solution)/shard_map/select/pallas_call | solution.py:244
  38.5 3.7 %all-to-all-start.1 = ((bf16[8,6,32,128]{3,2,1,0:T(8,128)(2,1)}), bf16[8,6,32,128]{3,2,1,0:T(8,128)(2,1)S(1)}, u32[]{:S(2)}, u32[]{:S(2)}) async-start(bf16[8,6,32,128]{3,2,1,0:T(8,128)(2,1)} %select.8), calls=%async_computation.1 | async-start | bytes 786432 | tf_op jit(solution)/shard_map/all_to_all | solution.py:252
  42.9 8.3 %all-to-all-done.1.sel = bf16[8,6,32,128]{3,2,1,0:T(8,128)(2,1)S(1)} async-done(((bf16[8,6,32,128]{3,2,1,0:T(8,128)(2,1)}), bf16[8,6,32,128]{3,2,1,0:T(8,128)(2,1)S(1)}, u32[]{:S(2)}, u32[]{:S(2)}) %all-to-all-start.1) | async-done | bytes 393248 | tf_op jit(solution)/shard_map/all_to_all | solution.py:252
  51.2 0.0 copy-done.1
  51.2 14.4 %contract.1 = f32[8,6,32,128]{3,2,1,0:T(8,128)S(1)} custom-call(s32[2,3]{1,0:T(2,128)S(1)} %copy-done.1, s32[1]{0:T(128)S(6)} %copy.29.count, bf16[2,128,128,128]{3,2,1,0:T(8,128)(2,1)} %x_far.1, bf16[8,6,32,128]{3,2,1,0:T(8,128)(2,1)S(1)} %all-to-all-done.1.sel), custom_call_target="tpu_custom_call" | custom-call | tf_op jit(solution)/shard_map/contract/pallas_call | solution.py:256
  65.6 15.6 %all_to_all.20.parts = f32[8,6,32,128]{3,2,1,0:T(8,128)S(1)} all-to-all(f32[8,6,32,128]{3,2,1,0:T(8,128)S(1)} %contract.1), channel_id=1, replica_groups=mesh['blk_0'=8,'blk_1'=4,'rep'=8] {'rep'}, dimensions={0} | all-to-all | bytes 1572864 | tf_op jit(solution)/shard_map/all_to_all | solution.py:283
  81.2 1.1 scatter.1
  82.3 0.9 convert_element_type.31
  83.2 5.6 %all-to-all-start.3 = ((f16[32,72,128]{2,1,0:T(8,128)(2,1)}), f16[32,72,128]{2,1,0:T(8,128)(2,1)S(1)}, u32[]{:S(2)}, u32[]{:S(2)}) async-start(f16[32,72,128]{2,1,0:T(8,128)(2,1)} %convert_element_type.31), calls=%async_computation.3 | async-start | bytes 1179648 | tf_op jit(solution)/shard_map/all_to_all | solution.py:305
  88.8 0.1 gram.1
  88.9 0.3 collective-permute-start.7
  89.2 4.1 %collective-permute-done.7 = f32[32,256]{1,0:T(8,128)S(1)} collective-permute-done((f32[32,256]{1,0:T(8,128)S(1)}, f32[32,256]{1,0:T(8,128)S(1)}, u32[]{:S(2)}, u32[]{:S(2)}) %collective-permute-start.7) | collective-permute-done | bytes 32800 | tf_op jit(solution)/shard_map/ppermute | solution.py:211
  93.3 2.5 %collective-permute-start.8 = (f32[32,256]{1,0:T(8,128)S(1)}, f32[32,256]{1,0:T(8,128)S(1)}, u32[]{:S(2)}, u32[]{:S(2)}) collective-permute-start(f32[32,256]{1,0:T(8,128)S(1)} %add.17), channel_id=1, source_target_pairs={{0,16},{8,24},{16,0},{24,8},{1,17},{9,25},{17,1},{25,9},{2,18},{10... | collective-permute-start | bytes 98312 | tf_op jit(solution)/shard_map/ppermute | solution.py:211
  95.8 3.0 %collective-permute-done.8 = f32[32,256]{1,0:T(8,128)S(1)} collective-permute-done((f32[32,256]{1,0:T(8,128)S(1)}, f32[32,256]{1,0:T(8,128)S(1)}, u32[]{:S(2)}, u32[]{:S(2)}) %collective-permute-start.8) | collective-permute-done | bytes 32800 | tf_op jit(solution)/shard_map/ppermute | solution.py:211
  98.8 2.6 %collective-permute-start.9 = (f32[32,256]{1,0:T(8,128)S(1)}, f32[32,256]{1,0:T(8,128)S(1)}, u32[]{:S(2)}, u32[]{:S(2)}) collective-permute-start(f32[32,256]{1,0:T(8,128)S(1)} %add.18), channel_id=1, source_target_pairs={{0,32},{32,0},{64,96},{96,64},{128,160},{160,128},{192,224},{224,1... | collective-permute-start | bytes 98312 | tf_op jit(solution)/shard_map/ppermute | solution.py:211
  101.4 2.0 %collective-permute-done.9 = f32[32,256]{1,0:T(8,128)S(1)} collective-permute-done((f32[32,256]{1,0:T(8,128)S(1)}, f32[32,256]{1,0:T(8,128)S(1)}, u32[]{:S(2)}, u32[]{:S(2)}) %collective-permute-start.9) | collective-permute-done | bytes 32800 | tf_op jit(solution)/shard_map/ppermute | solution.py:211
  103.4 2.3 %collective-permute-start.10 = (f32[32,256]{1,0:T(8,128)S(1)}, f32[32,256]{1,0:T(8,128)S(1)}, u32[]{:S(2)}, u32[]{:S(2)}) collective-permute-start(f32[32,256]{1,0:T(8,128)S(1)} %add.19), channel_id=1, source_target_pairs={{0,64},{32,96},{64,0},{96,32},{128,192},{160,224},{192,128},{224,1... | collective-permute-start | bytes 98312 | tf_op jit(solution)/shard_map/ppermute | solution.py:211
  105.8 2.5 %collective-permute-done.10 = f32[32,256]{1,0:T(8,128)S(1)} collective-permute-done((f32[32,256]{1,0:T(8,128)S(1)}, f32[32,256]{1,0:T(8,128)S(1)}, u32[]{:S(2)}, u32[]{:S(2)}) %collective-permute-start.10) | collective-permute-done | bytes 32800 | tf_op jit(solution)/shard_map/ppermute | solution.py:211
  108.2 5.0 %collective-permute-start.11 = (f32[32,256]{1,0:T(8,128)S(1)}, f32[32,256]{1,0:T(8,128)S(1)}, u32[]{:S(2)}, u32[]{:S(2)}) collective-permute-start(f32[32,256]{1,0:T(8,128)S(1)} %add.20), channel_id=1, source_target_pairs={{0,128},{32,160},{64,192},{96,224},{128,0},{160,32},{192,64},{224,... | collective-permute-start | bytes 98312 | tf_op jit(solution)/shard_map/ppermute | solution.py:211
  113.2 2.9 %collective-permute-done.11 = f32[32,256]{1,0:T(8,128)S(1)} collective-permute-done((f32[32,256]{1,0:T(8,128)S(1)}, f32[32,256]{1,0:T(8,128)S(1)}, u32[]{:S(2)}, u32[]{:S(2)}) %collective-permute-start.11) | collective-permute-done | bytes 32800 | tf_op jit(solution)/shard_map/ppermute | solution.py:211
  116.2 0.2 fit.1
  116.3 0.0 all-to-all-done.3
  116.4 0.1 convert_element_type.32
  116.4 0.3 fusion.5
  116.8 0.1 fusion
  116.9 0.6 bitcast_bitcast_fusion
  (17 shorter events, 0.1 us)
Async XLA Ops:
  0.0 0.8 copy-start
  0.8 24.3 %collective-permute-start.5 = (bf16[80,128]{1,0:T(8,128)(2,1)S(1)}, bf16[80,128]{1,0:T(8,128)(2,1)S(1)}, u32[]{:S(2)}, u32[]{:S(2)}) collective-permute-start(bf16[80,128]{1,0:T(8,128)(2,1)S(1)} %fusion.2), channel_id=1, source_target_pairs={{0,6},{1,7},{2,0},{3,1},{4,2},{5,3},{6,4},{7,5},{8,14},{9,15},{10,... | collective-permute-start | bytes 61448 | tf_op jit(solution)/shard_map/ppermute | solution.py:198
  3.6 21.4 %collective-permute-start.4 = (bf16[80,128]{1,0:T(8,128)(2,1)S(1)}, bf16[80,128]{1,0:T(8,128)(2,1)S(1)}, u32[]{:S(2)}, u32[]{:S(2)}) collective-permute-start(bf16[80,128]{1,0:T(8,128)(2,1)S(1)} %fusion.2), channel_id=1, source_target_pairs={{0,5},{1,6},{2,7},{3,0},{4,1},{5,2},{6,3},{7,4},{8,13},{9,14},{10,... | collective-permute-start | bytes 61448 | tf_op jit(solution)/shard_map/ppermute | solution.py:198
  3.6 21.4 %collective-permute-start.3 = (bf16[80,128]{1,0:T(8,128)(2,1)S(1)}, bf16[80,128]{1,0:T(8,128)(2,1)S(1)}, u32[]{:S(2)}, u32[]{:S(2)}) collective-permute-start(bf16[80,128]{1,0:T(8,128)(2,1)S(1)} %fusion.2), channel_id=1, source_target_pairs={{0,4},{1,5},{2,6},{3,7},{4,0},{5,1},{6,2},{7,3},{8,12},{9,13},{10,... | collective-permute-start | bytes 61448 | tf_op jit(solution)/shard_map/ppermute | solution.py:198
  6.3 18.7 %collective-permute-start.2 = (bf16[80,128]{1,0:T(8,128)(2,1)S(1)}, bf16[80,128]{1,0:T(8,128)(2,1)S(1)}, u32[]{:S(2)}, u32[]{:S(2)}) collective-permute-start(bf16[80,128]{1,0:T(8,128)(2,1)S(1)} %fusion.2), channel_id=1, source_target_pairs={{0,3},{1,4},{2,5},{3,6},{4,7},{5,0},{6,1},{7,2},{8,11},{9,12},{10,... | collective-permute-start | bytes 61448 | tf_op jit(solution)/shard_map/ppermute | solution.py:198
  6.3 13.6 %collective-permute-start = (bf16[80,128]{1,0:T(8,128)(2,1)S(1)}, bf16[80,128]{1,0:T(8,128)(2,1)S(1)}, u32[]{:S(2)}, u32[]{:S(2)}) collective-permute-start(bf16[80,128]{1,0:T(8,128)(2,1)S(1)} %fusion.2), channel_id=1, source_target_pairs={{0,1},{1,2},{2,3},{3,4},{4,5},{5,6},{6,7},{7,0},{8,9},{9,10},{10,1... | collective-permute-start | bytes 61448 | tf_op jit(solution)/shard_map/ppermute | solution.py:198
  8.2 28.9 %all-to-all-start = ((bf16[32,2,32,128]{3,2,1,0:T(8,128)(2,1)}), bf16[32,2,32,128]{3,2,1,0:T(8,128)(2,1)S(1)}, u32[]{:S(2)}, u32[]{:S(2)}) async-start(bf16[32,2,32,128]{3,2,1,0:T(8,128)(2,1)} %broadcast_in_dim.2), calls=%async_computation | async-start | bytes 1048576 | tf_op jit(solution)/shard_map/all_to_all | solution.py:227
  19.9 31.3 %copy-start.1 = (s32[2,3]{1,0:T(2,128)S(1)}, s32[2,3]{1,0:T(2,128)}, u32[]{:S(2)}) copy-start(s32[2,3]{1,0:T(2,128)} %triples.1) | copy-start | bytes 76
  20.0 5.1 %collective-permute-start.1 = (bf16[80,128]{1,0:T(8,128)(2,1)S(1)}, bf16[80,128]{1,0:T(8,128)(2,1)S(1)}, u32[]{:S(2)}, u32[]{:S(2)}) collective-permute-start(bf16[80,128]{1,0:T(8,128)(2,1)S(1)} %fusion.2), channel_id=1, source_target_pairs={{0,2},{1,3},{2,4},{3,5},{4,6},{5,7},{6,0},{7,1},{8,10},{9,11},{10,... | collective-permute-start | bytes 61448 | tf_op jit(solution)/shard_map/ppermute | solution.py:198
  25.0 1.5 %collective-permute-start.6 = (bf16[80,128]{1,0:T(8,128)(2,1)S(1)}, bf16[80,128]{1,0:T(8,128)(2,1)S(1)}, u32[]{:S(2)}, u32[]{:S(2)}) collective-permute-start(bf16[80,128]{1,0:T(8,128)(2,1)S(1)} %fusion.2), channel_id=1, source_target_pairs={{0,7},{1,0},{2,1},{3,2},{4,3},{5,4},{6,5},{7,6},{8,15},{9,8},{10,9... | collective-permute-start | bytes 61448 | tf_op jit(solution)/shard_map/ppermute | solution.py:198
  38.5 12.7 %all-to-all-start.1 = ((bf16[8,6,32,128]{3,2,1,0:T(8,128)(2,1)}), bf16[8,6,32,128]{3,2,1,0:T(8,128)(2,1)S(1)}, u32[]{:S(2)}, u32[]{:S(2)}) async-start(bf16[8,6,32,128]{3,2,1,0:T(8,128)(2,1)} %select.8), calls=%async_computation.1 | async-start | bytes 786432 | tf_op jit(solution)/shard_map/all_to_all | solution.py:252
  83.2 33.2 %all-to-all-start.3 = ((f16[32,72,128]{2,1,0:T(8,128)(2,1)}), f16[32,72,128]{2,1,0:T(8,128)(2,1)S(1)}, u32[]{:S(2)}, u32[]{:S(2)}) async-start(f16[32,72,128]{2,1,0:T(8,128)(2,1)} %convert_element_type.31), calls=%async_computation.3 | async-start | bytes 1179648 | tf_op jit(solution)/shard_map/all_to_all | solution.py:305
  88.9 4.4 %collective-permute-start.7 = (f32[32,256]{1,0:T(8,128)S(1)}, f32[32,256]{1,0:T(8,128)S(1)}, u32[]{:S(2)}, u32[]{:S(2)}) collective-permute-start(f32[32,256]{1,0:T(8,128)S(1)} %gram.1), channel_id=1, source_target_pairs={{0,8},{8,0},{16,24},{24,16},{1,9},{9,1},{17,25},{25,17},{2,10},{10... | collective-permute-start | bytes 98312 | tf_op jit(solution)/shard_map/ppermute | solution.py:211
  93.3 5.4 %collective-permute-start.8 = (f32[32,256]{1,0:T(8,128)S(1)}, f32[32,256]{1,0:T(8,128)S(1)}, u32[]{:S(2)}, u32[]{:S(2)}) collective-permute-start(f32[32,256]{1,0:T(8,128)S(1)} %add.17), channel_id=1, source_target_pairs={{0,16},{8,24},{16,0},{24,8},{1,17},{9,25},{17,1},{25,9},{2,18},{10... | collective-permute-start | bytes 98312 | tf_op jit(solution)/shard_map/ppermute | solution.py:211
  98.8 4.6 %collective-permute-start.9 = (f32[32,256]{1,0:T(8,128)S(1)}, f32[32,256]{1,0:T(8,128)S(1)}, u32[]{:S(2)}, u32[]{:S(2)}) collective-permute-start(f32[32,256]{1,0:T(8,128)S(1)} %add.18), channel_id=1, source_target_pairs={{0,32},{32,0},{64,96},{96,64},{128,160},{160,128},{192,224},{224,1... | collective-permute-start | bytes 98312 | tf_op jit(solution)/shard_map/ppermute | solution.py:211
  103.4 4.8 %collective-permute-start.10 = (f32[32,256]{1,0:T(8,128)S(1)}, f32[32,256]{1,0:T(8,128)S(1)}, u32[]{:S(2)}, u32[]{:S(2)}) collective-permute-start(f32[32,256]{1,0:T(8,128)S(1)} %add.19), channel_id=1, source_target_pairs={{0,64},{32,96},{64,0},{96,32},{128,192},{160,224},{192,128},{224,1... | collective-permute-start | bytes 98312 | tf_op jit(solution)/shard_map/ppermute | solution.py:211
  108.2 7.9 %collective-permute-start.11 = (f32[32,256]{1,0:T(8,128)S(1)}, f32[32,256]{1,0:T(8,128)S(1)}, u32[]{:S(2)}, u32[]{:S(2)}) collective-permute-start(f32[32,256]{1,0:T(8,128)S(1)} %add.20), channel_id=1, source_target_pairs={{0,128},{32,160},{64,192},{96,224},{128,0},{160,32},{192,64},{224,... | collective-permute-start | bytes 98312 | tf_op jit(solution)/shard_map/ppermute | solution.py:211

commit v2 on v1

--- a/solution.py
+++ b/solution.py
@@ -33,7 +33,7 @@
 def select_kernel(names, place, table, out):
     reps, named = names.shape
     for peer in range(reps):
-        back = lax.rem(place[0] + reps - peer, reps)
+        back = jnp.bitwise_xor(place[0], peer)
         for t in range(named):
             out[peer, t] = table[names[back, t]]
 
@@ -159,6 +159,8 @@
 
     lax.fori_loop(0, pieces, several, 0)
 
+    scaled = []
+    top = jnp.zeros((1, 1), F32)
     for slot in range(slots):
         i, j, k = triples[slot, 0], triples[slot, 1], triples[slot, 2]
         upper_tie = i == j
@@ -166,50 +168,67 @@
         alive = jnp.where(slot < count[0], 1.0, 0.0)
         base = jnp.where(upper_tie | lower_tie, 1.0, 2.0) * alive
         dropped = jnp.where(upper_tie & lower_tie, 0.0, base)
-        for side, (value, weight) in enumerate(((y1, base), (y2, dropped), (y3, dropped))):
-            out[:, slot * 3 + side] = (value[slot].T * weight).reshape(reps, width, BS)
+        for value, weight in ((y1, base), (y2, dropped), (y3, dropped)):
+            scaled.append((value, slot, weight))
+            top = jnp.maximum(top, top_of(value[slot]) * weight)
+    power = power_of(top)
+    scale = stretched(jnp.exp2(power), rank)
+    for t, (value, slot, weight) in enumerate(scaled):
+        out[:, t * width : (t + 1) * width] = (value[slot].T * (scale * weight)).reshape(
+            reps, width, BS
+        )
+    for peer in range(reps):
+        out[peer, len(scaled) * width :] = power
+
+
+def power_of(top):
+    power = 14.0 - jnp.ceil(jnp.log2(jnp.maximum(top, 1e-36)))
+    return jnp.broadcast_to(jnp.clip(power, -120.0, 120.0), (SUBLANES, BS))
+
+
+def stretched(row, count):
+    return jnp.concatenate([row] * (count // SUBLANES), axis=0)
+
+
+def top_of(value):
+    return jnp.max(jnp.max(jnp.abs(value), axis=0, keepdims=True), axis=1, keepdims=True)
 
 
 def scatter_kernel(names, place, parts, out, total):
     reps, named = names.shape
     owners = out.shape[0]
-    width = parts.shape[2]
     per_owner = total.shape[0] // owners
+    width = total.shape[1]
     total[...] = jnp.zeros_like(total)
     for peer in range(reps):
-        back = lax.rem(place[0] + reps - peer, reps)
+        back = jnp.bitwise_xor(place[0], peer)
+        undo = stretched(jnp.exp2(-parts[peer, named * width :]), width)
         for t in range(named):
             at = names[back, t]
-            total[at] = total[at] + parts[peer, t]
-    top = jnp.max(jnp.abs(total[...]), axis=(0, 1), keepdims=True)[0]
-    top = jnp.max(top, axis=1, keepdims=True)
-    power = jnp.clip(14.0 - jnp.ceil(jnp.log2(jnp.maximum(top, 1e-36))), -100.0, 100.0)
-    power = jnp.broadcast_to(power, (SUBLANES, BS))
-    scale = jnp.exp2(power)
-    scale = jnp.concatenate([scale] * (width // SUBLANES), axis=0)
+            total[at] = total[at] + parts[peer, t * width : (t + 1) * width] * undo
+    power = power_of(top_of(jnp.max(jnp.abs(total[...]), axis=0)))
+    scale = stretched(jnp.exp2(power), width)
     for owner in range(owners):
         for t in range(per_owner):
             out[owner, t * width : (t + 1) * width] = total[owner * per_owner + t] * scale
         out[owner, per_owner * width :] = power
 
 
-def moved(array, axis, shift):
+def swapped(array, axis, bit):
     peers = lax.axis_size(axis)
-    return lax.ppermute(array, axis, [(i, (i + shift) % peers) for i in range(peers)])
+    return lax.ppermute(array, axis, [(i, i ^ bit) for i in range(peers)])
 
 
 def from_each(array, axis):
-    peers = lax.axis_size(axis)
-    return jnp.stack([array] + [moved(array, axis, shift) for shift in range(1, peers)])
-
-
-def summed(array, axis):
-    peers = lax.axis_size(axis)
-    bit = 1
-    while bit < peers:
-        swap = [(i, i ^ bit) for i in range(peers)]
-        array = array + lax.ppermute(array, axis, swap)
-        bit *= 2
+    array = array[None]
+    while array.shape[0] < lax.axis_size(axis):
+        array = jnp.concatenate([array, swapped(array, axis, array.shape[0])])
+    return array
+
+
+def summed(array, axis, bits):
+    for bit in bits:
+        array = array + swapped(array, axis, bit)
     return array
 
 
@@ -251,11 +270,12 @@
     )(names, place, near(table))
     chosen = lax.all_to_all(chosen, "rep", 0, 0, tiled=True)
 
-    gram = summed(gram, "blk_1")
+    gram = summed(gram, "blk_1", (1, 2))
+    gram = summed(gram, "blk_0", (4,))
 
     parts = pl.pallas_call(
         contract_kernel,
-        out_shape=VMEM((reps, named, width, BS), F32),
+        out_shape=VMEM((reps, named * width + SUBLANES, BS), F32),
         in_specs=[whole(SMEM), whole(SMEM), whole(pltpu.HBM), whole()],
         out_specs=whole(),
         scratch_shapes=[
@@ -280,9 +300,9 @@
         pltpu.with_memory_space_constraint(tensor_blocks, pltpu.HBM),
         near(chosen),
     )
-    parts = lax.all_to_all(parts, "rep", 0, 0, tiled=True)
-
-    gram = summed(gram, "blk_0")
+    parts = lax.all_to_all(parts.astype(F16), "rep", 0, 0, tiled=True)
+
+    gram = summed(gram, "blk_0", (1, 2))
     fitted = pl.pallas_call(
         fit_kernel,
         out_shape=jax.ShapeDtypeStruct((per_owner, width, BS), F32),
@@ -301,7 +321,7 @@
         scratch_shapes=[VMEM((owners * per_owner, width, BS), F32)],
         compiler_params=pltpu.CompilerParams(vmem_limit_bytes=16 << 20),
         name="scatter",
-    )(names, place, near(parts))
+    )(names, place, near(parts.astype(F32)))
     arrived = lax.all_to_all(scaled.astype(F16), BLK, 0, 0, tiled=True)
     arrived = arrived.astype(F32)
     moment = (arrived[:, :held] * jnp.exp2(-arrived[:, held:, :1][:, :1])).sum(0)

time: 118 us -> 108 us (0.915)
  blocking collectives: 15.6 us -> 11.5 us
  starting transfers between devices: 41.1 us -> 37.8 us
  waiting for transfers between devices: 38.9 us -> 36.3 us
    all_to_all x1, waiting for transfers between devices: 10.6 us -> 5.4 us  [shards(): lax.all_to_all(jnp.broadcast_to(own[None], (owners, *own.shape)), BLK, 0,...]
    all_to_all x1, blocking collectives: 15.6 us -> 11.5 us  [shards(): parts = lax.all_to_all(parts.astype(F16), 'rep', 0, 0, tiled=True)]
    ppermute x12 -> x8, starting transfers between devices: 20.1 us -> 16.2 us  [swapped(): return lax.ppermute(array, axis, [(i, i ^ bit) for i in range(peers)])]
    ppermute x12 -> x8, waiting for transfers between devices: 20.1 us -> 22.7 us  [swapped(): return lax.ppermute(array, axis, [(i, i ^ bit) for i in range(peers)])]
  transfers between devices with their start and end apart: 15 -> 11, of which waited for: 9 -> 10; matrix products, arithmetic and copies ran while one was open for 1% -> 0% of each run, Pallas kernels for 0% -> 0%
where the time goes in v2:
time: 108 us
  starting transfers between devices  37.8 us (35%)
  waiting for transfers between devices  36.3 us (34%)
  Pallas kernels  17.3 us (16%)
  blocking collectives  11.5 us (11%)
  other arithmetic  2.25 us (2%)
  local copies, waits for them, and re-layouts  1.73 us (2%)
    ppermute x8, waiting for transfers between devices, swapped(): return lax.ppermute(array, axis, [(i, i ^ bit) for i in range(peers)])  22.7 us
    ppermute x8, starting transfers between devices, swapped(): return lax.ppermute(array, axis, [(i, i ^ bit) for i in range(peers)])  16.2 us
    pallas_call x1, Pallas kernels, shards(): pl.pallas_call(contract_kernel, out_shape=VMEM((reps, named * width + SUB...  14.5 us
    all_to_all x1, starting transfers between devices, shards(): lax.all_to_all(jnp.broadcast_to(own[None], (owners, *own.shape)), BLK, 0,...  11.7 us
    all_to_all x1, blocking collectives, shards(): parts = lax.all_to_all(parts.astype(F16), 'rep', 0, 0, tiled=True)  11.5 us
    all_to_all x1, waiting for transfers between devices, shards(): chosen = lax.all_to_all(chosen, 'rep', 0, 0, tiled=True)  8.26 us
    all_to_all x1, starting transfers between devices, shards(): arrived = lax.all_to_all(scaled.astype(F16), BLK, 0, 0, tiled=True)  5.57 us
    all_to_all x1, waiting for transfers between devices, shards(): lax.all_to_all(jnp.broadcast_to(own[None], (owners, *own.shape)), BLK, 0,...  5.4 us
  transfers between devices with their start and end apart: 11, of which 10 were waited for; matrix products, arithmetic and copies ran while one was open for 0% of the time, Pallas kernels for 0%

profile of v2, /device:TPU:8, one launch (start us, length us, event | category | flops | bytes accessed | tf_op | source)
XLA Modules:
  0.0 107.6 jit_solution(3818430679445885123)
XLA Ops:
  0.0 0.0 copy-start
  0.0 0.0 copy-start.1
  0.0 0.7 copy-done
  0.7 0.9 broadcast_in_dim.10
  1.6 11.7 %all-to-all-start = ((bf16[32,2,32,128]{3,2,1,0:T(8,128)(2,1)}), bf16[32,2,32,128]{3,2,1,0:T(8,128)(2,1)S(1)}, u32[]{:S(2)}, u32[]{:S(2)}) async-start(bf16[32,2,32,128]{3,2,1,0:T(8,128)(2,1)} %broadcast_in_dim.10), calls=%async_computation | async-start | bytes 1048576 | tf_op jit(solution)/shard_map/all_to_all | solution.py:246
  13.3 0.0 copy-done.1
  13.4 0.1 convert_element_type.34
  13.5 0.1 collective-permute-start
  13.5 1.2 %collective-permute-done = bf16[1,80,128]{2,1,0:T(8,128)(2,1)S(1)} collective-permute-done((bf16[1,80,128]{2,1,0:T(8,128)(2,1)S(1)}, bf16[1,80,128]{2,1,0:T(8,128)(2,1)S(1)}, u32[]{:S(2)}, u32[]{:S(2)}) %collective-permute-start) | collective-permute-done | bytes 20512 | tf_op jit(solution)/shard_map/ppermute | solution.py:219
  14.7 1.5 %collective-permute-start.1 = (bf16[2,80,128]{2,1,0:T(8,128)(2,1)S(1)}, bf16[2,80,128]{2,1,0:T(8,128)(2,1)S(1)}, u32[]{:S(2)}, u32[]{:S(2)}) collective-permute-start(bf16[2,80,128]{2,1,0:T(8,128)(2,1)S(1)} %pad_maximum_fusion.2), channel_id=1, source_target_pairs={{0,2},{1,3},{2,0},{3,1},{4,6},{5,7},{6,4},{7,5},{8,10},{9,11},{10,... | collective-permute-start | bytes 122888 | tf_op jit(solution)/shard_map/ppermute | solution.py:219
  16.2 2.5 %collective-permute-done.1 = bf16[2,80,128]{2,1,0:T(8,128)(2,1)S(1)} collective-permute-done((bf16[2,80,128]{2,1,0:T(8,128)(2,1)S(1)}, bf16[2,80,128]{2,1,0:T(8,128)(2,1)S(1)}, u32[]{:S(2)}, u32[]{:S(2)}) %collective-permute-start.1) | collective-permute-done | bytes 40992 | tf_op jit(solution)/shard_map/ppermute | solution.py:219
  18.7 3.1 %collective-permute-start.2 = (bf16[4,80,128]{2,1,0:T(8,128)(2,1)S(1)}, bf16[4,80,128]{2,1,0:T(8,128)(2,1)S(1)}, u32[]{:S(2)}, u32[]{:S(2)}) collective-permute-start(bf16[4,80,128]{2,1,0:T(8,128)(2,1)S(1)} %pad_maximum_fusion.1), channel_id=1, source_target_pairs={{0,4},{1,5},{2,6},{3,7},{4,0},{5,1},{6,2},{7,3},{8,12},{9,13},{10,... | collective-permute-start | bytes 245768 | tf_op jit(solution)/shard_map/ppermute | solution.py:219
  21.8 2.9 %collective-permute-done.2 = bf16[4,80,128]{2,1,0:T(8,128)(2,1)S(1)} collective-permute-done((bf16[4,80,128]{2,1,0:T(8,128)(2,1)S(1)}, bf16[4,80,128]{2,1,0:T(8,128)(2,1)S(1)}, u32[]{:S(2)}, u32[]{:S(2)}) %collective-permute-start.2) | collective-permute-done | bytes 81952 | tf_op jit(solution)/shard_map/ppermute | solution.py:219
  24.8 5.4 %all-to-all-done = bf16[32,2,32,128]{3,2,1,0:T(8,128)(2,1)S(1)} async-done(((bf16[32,2,32,128]{3,2,1,0:T(8,128)(2,1)}), bf16[32,2,32,128]{3,2,1,0:T(8,128)(2,1)S(1)}, u32[]{:S(2)}, u32[]{:S(2)}) %all-to-all-start) | async-done | bytes 524320 | tf_op jit(solution)/shard_map/all_to_all | solution.py:246
  30.2 1.4 %select.8 = bf16[8,6,32,128]{3,2,1,0:T(8,128)(2,1)} custom-call(s32[8,6]{1,0:T(8,128)S(1)} %bitcast.30, s32[1]{0:T(128)} %bitcast.6.place, bf16[64,32,128]{2,1,0:T(8,128)(2,1)S(1)} %bitcast.27), custom_call_target="tpu_custom_call" | custom-call | tf_op jit(solution)/shard_map/select/pallas_call | solution.py:263
  31.6 4.3 %all-to-all-start.1 = ((bf16[8,6,32,128]{3,2,1,0:T(8,128)(2,1)}), bf16[8,6,32,128]{3,2,1,0:T(8,128)(2,1)S(1)}, u32[]{:S(2)}, u32[]{:S(2)}) async-start(bf16[8,6,32,128]{3,2,1,0:T(8,128)(2,1)} %select.8), calls=%async_computation.1 | async-start | bytes 786432 | tf_op jit(solution)/shard_map/all_to_all | solution.py:271
  36.5 8.3 %all-to-all-done.1.sel = bf16[8,6,32,128]{3,2,1,0:T(8,128)(2,1)S(1)} async-done(((bf16[8,6,32,128]{3,2,1,0:T(8,128)(2,1)}), bf16[8,6,32,128]{3,2,1,0:T(8,128)(2,1)S(1)}, u32[]{:S(2)}, u32[]{:S(2)}) %all-to-all-start.1) | async-done | bytes 393248 | tf_op jit(solution)/shard_map/all_to_all | solution.py:271
  44.8 14.5 %contract.1 = f32[8,200,128]{2,1,0:T(8,128)S(1)} custom-call(s32[2,3]{1,0:T(2,128)S(1)} %copy-done.1, s32[1]{0:T(128)S(6)} %copy.15.count, bf16[2,128,128,128]{3,2,1,0:T(8,128)(2,1)} %x_far.1, bf16[8,6,32,128]{3,2,1,0:T(8,128)(2,1)S(1)} %all-to-all-done.1.sel), custom_call_target="tpu_custom_call" | custom-call | tf_op jit(solution)/shard_map/contract/pallas_call | solution.py:276
  59.3 0.1 convert_element_type.37
  59.3 11.5 %all_to_all.20 = f16[8,200,128]{2,1,0:T(8,128)(2,1)S(1)} all-to-all(f16[8,200,128]{2,1,0:T(8,128)(2,1)S(1)} %convert_element_type.37), channel_id=1, replica_groups=mesh['blk_0'=8,'blk_1'=4,'rep'=8] {'rep'}, dimensions={0} | all-to-all | bytes 819200 | tf_op jit(solution)/shard_map/all_to_all | solution.py:303
  70.8 0.1 convert_element_type.38.parts
  70.9 1.1 %scatter.1 = f32[32,72,128]{2,1,0:T(8,128)S(1)} custom-call(s32[8,6]{1,0:T(8,128)S(1)} %bitcast.31, s32[1]{0:T(128)} %bitcast.6.place, f32[8,200,128]{2,1,0:T(8,128)S(1)} %convert_element_type.38.parts), custom_call_target="tpu_custom_call" | custom-call | tf_op jit(solution)/shard_map/scatter/pallas_call | solution.py:316
  72.0 0.9 convert_element_type.39
  72.9 5.6 %all-to-all-start.3 = ((f16[32,72,128]{2,1,0:T(8,128)(2,1)}), f16[32,72,128]{2,1,0:T(8,128)(2,1)S(1)}, u32[]{:S(2)}, u32[]{:S(2)}) async-start(f16[32,72,128]{2,1,0:T(8,128)(2,1)} %convert_element_type.39), calls=%async_computation.3 | async-start | bytes 1179648 | tf_op jit(solution)/shard_map/all_to_all | solution.py:325
  78.5 0.1 gram.1
  78.6 0.3 collective-permute-start.3
  78.9 4.0 %collective-permute-done.3 = f32[32,256]{1,0:T(8,128)S(1)} collective-permute-done((f32[32,256]{1,0:T(8,128)S(1)}, f32[32,256]{1,0:T(8,128)S(1)}, u32[]{:S(2)}, u32[]{:S(2)}) %collective-permute-start.3) | collective-permute-done | bytes 32800 | tf_op jit(solution)/shard_map/ppermute | solution.py:219
  83.0 2.6 %collective-permute-start.4 = (f32[32,256]{1,0:T(8,128)S(1)}, f32[32,256]{1,0:T(8,128)S(1)}, u32[]{:S(2)}, u32[]{:S(2)}) collective-permute-start(f32[32,256]{1,0:T(8,128)S(1)} %add.17), channel_id=1, source_target_pairs={{0,16},{8,24},{16,0},{24,8},{1,17},{9,25},{17,1},{25,9},{2,18},{10... | collective-permute-start | bytes 98312 | tf_op jit(solution)/shard_map/ppermute | solution.py:219
  85.5 2.9 %collective-permute-done.4 = f32[32,256]{1,0:T(8,128)S(1)} collective-permute-done((f32[32,256]{1,0:T(8,128)S(1)}, f32[32,256]{1,0:T(8,128)S(1)}, u32[]{:S(2)}, u32[]{:S(2)}) %collective-permute-start.4) | collective-permute-done | bytes 32800 | tf_op jit(solution)/shard_map/ppermute | solution.py:219
  88.4 5.7 %collective-permute-start.5 = (f32[32,256]{1,0:T(8,128)S(1)}, f32[32,256]{1,0:T(8,128)S(1)}, u32[]{:S(2)}, u32[]{:S(2)}) collective-permute-start(f32[32,256]{1,0:T(8,128)S(1)} %add.18), channel_id=1, source_target_pairs={{0,128},{32,160},{64,192},{96,224},{128,0},{160,32},{192,64},{224,... | collective-permute-start | bytes 98312 | tf_op jit(solution)/shard_map/ppermute | solution.py:219
  94.1 3.4 %collective-permute-done.5 = f32[32,256]{1,0:T(8,128)S(1)} collective-permute-done((f32[32,256]{1,0:T(8,128)S(1)}, f32[32,256]{1,0:T(8,128)S(1)}, u32[]{:S(2)}, u32[]{:S(2)}) %collective-permute-start.5) | collective-permute-done | bytes 32800 | tf_op jit(solution)/shard_map/ppermute | solution.py:219
  97.5 1.3 %collective-permute-start.6 = (f32[32,256]{1,0:T(8,128)S(1)}, f32[32,256]{1,0:T(8,128)S(1)}, u32[]{:S(2)}, u32[]{:S(2)}) collective-permute-start(f32[32,256]{1,0:T(8,128)S(1)} %add.19), channel_id=1, source_target_pairs={{0,32},{32,0},{64,96},{96,64},{128,160},{160,128},{192,224},{224,1... | collective-permute-start | bytes 98312 | tf_op jit(solution)/shard_map/ppermute | solution.py:219
  98.8 2.6 %collective-permute-done.6 = f32[32,256]{1,0:T(8,128)S(1)} collective-permute-done((f32[32,256]{1,0:T(8,128)S(1)}, f32[32,256]{1,0:T(8,128)S(1)}, u32[]{:S(2)}, u32[]{:S(2)}) %collective-permute-start.6) | collective-permute-done | bytes 32800 | tf_op jit(solution)/shard_map/ppermute | solution.py:219
  101.4 1.6 %collective-permute-start.7 = (f32[32,256]{1,0:T(8,128)S(1)}, f32[32,256]{1,0:T(8,128)S(1)}, u32[]{:S(2)}, u32[]{:S(2)}) collective-permute-start(f32[32,256]{1,0:T(8,128)S(1)} %add.20), channel_id=1, source_target_pairs={{0,64},{32,96},{64,0},{96,32},{128,192},{160,224},{192,128},{224,1... | collective-permute-start | bytes 98312 | tf_op jit(solution)/shard_map/ppermute | solution.py:219
  103.1 3.2 %collective-permute-done.7 = f32[32,256]{1,0:T(8,128)S(1)} collective-permute-done((f32[32,256]{1,0:T(8,128)S(1)}, f32[32,256]{1,0:T(8,128)S(1)}, u32[]{:S(2)}, u32[]{:S(2)}) %collective-permute-start.7) | collective-permute-done | bytes 32800 | tf_op jit(solution)/shard_map/ppermute | solution.py:219
  106.3 0.2 fit.1
  106.4 0.0 all-to-all-done.3
  106.5 0.1 convert_element_type.40
  106.5 0.3 fusion.6
  106.9 0.1 fusion
  107.0 0.6 bitcast_bitcast_fusion
  (13 shorter events, 0.1 us)
Async XLA Ops:
  0.0 0.7 copy-start
  0.0 13.3 %copy-start.1 = (s32[2,3]{1,0:T(2,128)S(1)}, s32[2,3]{1,0:T(2,128)}, u32[]{:S(2)}) copy-start(s32[2,3]{1,0:T(2,128)} %triples.1) | copy-start | bytes 76
  1.6 28.5 %all-to-all-start = ((bf16[32,2,32,128]{3,2,1,0:T(8,128)(2,1)}), bf16[32,2,32,128]{3,2,1,0:T(8,128)(2,1)S(1)}, u32[]{:S(2)}, u32[]{:S(2)}) async-start(bf16[32,2,32,128]{3,2,1,0:T(8,128)(2,1)} %broadcast_in_dim.10), calls=%async_computation | async-start | bytes 1048576 | tf_op jit(solution)/shard_map/all_to_all | solution.py:246
  13.5 1.2 %collective-permute-start = (bf16[1,80,128]{2,1,0:T(8,128)(2,1)S(1)}, bf16[1,80,128]{2,1,0:T(8,128)(2,1)S(1)}, u32[]{:S(2)}, u32[]{:S(2)}) collective-permute-start(bf16[1,80,128]{2,1,0:T(8,128)(2,1)S(1)} %fusion.3), channel_id=1, source_target_pairs={{0,1},{1,0},{2,3},{3,2},{4,5},{5,4},{6,7},{7,6},{8,9},{9,8},{10,11... | collective-permute-start | bytes 61448 | tf_op jit(solution)/shard_map/ppermute | solution.py:219
  14.7 4.0 %collective-permute-start.1 = (bf16[2,80,128]{2,1,0:T(8,128)(2,1)S(1)}, bf16[2,80,128]{2,1,0:T(8,128)(2,1)S(1)}, u32[]{:S(2)}, u32[]{:S(2)}) collective-permute-start(bf16[2,80,128]{2,1,0:T(8,128)(2,1)S(1)} %pad_maximum_fusion.2), channel_id=1, source_target_pairs={{0,2},{1,3},{2,0},{3,1},{4,6},{5,7},{6,4},{7,5},{8,10},{9,11},{10,... | collective-permute-start | bytes 122888 | tf_op jit(solution)/shard_map/ppermute | solution.py:219
  18.7 6.0 %collective-permute-start.2 = (bf16[4,80,128]{2,1,0:T(8,128)(2,1)S(1)}, bf16[4,80,128]{2,1,0:T(8,128)(2,1)S(1)}, u32[]{:S(2)}, u32[]{:S(2)}) collective-permute-start(bf16[4,80,128]{2,1,0:T(8,128)(2,1)S(1)} %pad_maximum_fusion.1), channel_id=1, source_target_pairs={{0,4},{1,5},{2,6},{3,7},{4,0},{5,1},{6,2},{7,3},{8,12},{9,13},{10,... | collective-permute-start | bytes 245768 | tf_op jit(solution)/shard_map/ppermute | solution.py:219
  31.6 13.2 %all-to-all-start.1 = ((bf16[8,6,32,128]{3,2,1,0:T(8,128)(2,1)}), bf16[8,6,32,128]{3,2,1,0:T(8,128)(2,1)S(1)}, u32[]{:S(2)}, u32[]{:S(2)}) async-start(bf16[8,6,32,128]{3,2,1,0:T(8,128)(2,1)} %select.8), calls=%async_computation.1 | async-start | bytes 786432 | tf_op jit(solution)/shard_map/all_to_all | solution.py:271
  72.9 33.6 %all-to-all-start.3 = ((f16[32,72,128]{2,1,0:T(8,128)(2,1)}), f16[32,72,128]{2,1,0:T(8,128)(2,1)S(1)}, u32[]{:S(2)}, u32[]{:S(2)}) async-start(f16[32,72,128]{2,1,0:T(8,128)(2,1)} %convert_element_type.39), calls=%async_computation.3 | async-start | bytes 1179648 | tf_op jit(solution)/shard_map/all_to_all | solution.py:325
  78.6 4.3 %collective-permute-start.3 = (f32[32,256]{1,0:T(8,128)S(1)}, f32[32,256]{1,0:T(8,128)S(1)}, u32[]{:S(2)}, u32[]{:S(2)}) collective-permute-start(f32[32,256]{1,0:T(8,128)S(1)} %gram.1), channel_id=1, source_target_pairs={{0,8},{8,0},{16,24},{24,16},{1,9},{9,1},{17,25},{25,17},{2,10},{10... | collective-permute-start | bytes 98312 | tf_op jit(solution)/shard_map/ppermute | solution.py:219
  83.0 5.4 %collective-permute-start.4 = (f32[32,256]{1,0:T(8,128)S(1)}, f32[32,256]{1,0:T(8,128)S(1)}, u32[]{:S(2)}, u32[]{:S(2)}) collective-permute-start(f32[32,256]{1,0:T(8,128)S(1)} %add.17), channel_id=1, source_target_pairs={{0,16},{8,24},{16,0},{24,8},{1,17},{9,25},{17,1},{25,9},{2,18},{10... | collective-permute-start | bytes 98312 | tf_op jit(solution)/shard_map/ppermute | solution.py:219
  88.4 9.1 %collective-permute-start.5 = (f32[32,256]{1,0:T(8,128)S(1)}, f32[32,256]{1,0:T(8,128)S(1)}, u32[]{:S(2)}, u32[]{:S(2)}) collective-permute-start(f32[32,256]{1,0:T(8,128)S(1)} %add.18), channel_id=1, source_target_pairs={{0,128},{32,160},{64,192},{96,224},{128,0},{160,32},{192,64},{224,... | collective-permute-start | bytes 98312 | tf_op jit(solution)/shard_map/ppermute | solution.py:219
  97.5 3.9 %collective-permute-start.6 = (f32[32,256]{1,0:T(8,128)S(1)}, f32[32,256]{1,0:T(8,128)S(1)}, u32[]{:S(2)}, u32[]{:S(2)}) collective-permute-start(f32[32,256]{1,0:T(8,128)S(1)} %add.19), channel_id=1, source_target_pairs={{0,32},{32,0},{64,96},{96,64},{128,160},{160,128},{192,224},{224,1... | collective-permute-start | bytes 98312 | tf_op jit(solution)/shard_map/ppermute | solution.py:219
  101.4 4.8 %collective-permute-start.7 = (f32[32,256]{1,0:T(8,128)S(1)}, f32[32,256]{1,0:T(8,128)S(1)}, u32[]{:S(2)}, u32[]{:S(2)}) collective-permute-start(f32[32,256]{1,0:T(8,128)S(1)} %add.20), channel_id=1, source_target_pairs={{0,64},{32,96},{64,0},{96,32},{128,192},{160,224},{192,128},{224,1... | collective-permute-start | bytes 98312 | tf_op jit(solution)/shard_map/ppermute | solution.py:219

commit v3 on v2

--- a/solution.py
+++ b/solution.py
@@ -13,7 +13,8 @@
 BS = 128
 CHUNK = 8
 SUBLANES = 8
-STEP = 4
+STEP = 8
+PIECE = 4
 AHEAD = 3
 F32 = jnp.float32
 BF16 = jnp.bfloat16
@@ -67,7 +68,7 @@
 
 
 def fetch(source, target, arrived, piece):
-    held = STEP * CHUNK
+    held = PIECE * CHUNK
     per_slot = BS // held
     slot = piece // per_slot
     rows = pl.ds((piece - slot * per_slot) * held, held)
@@ -83,7 +84,7 @@
     rank = reps * width
     per_slot = BS // CHUNK
     chunks = slots * per_slot
-    pieces = chunks // STEP
+    pieces = chunks // PIECE
     for piece in range(min(AHEAD, pieces)):
         fetch(x_far, x, arrived, piece).start()
     for slot in range(slots):
@@ -140,13 +141,16 @@
     multiply(0, lower_a, middle_a)
 
     def several(step, carry):
-        @pl.when(step + AHEAD < pieces)
-        def _():
-            fetch(x_far, x, arrived, step + AHEAD).start()
-
-        @pl.when(step + 1 < pieces)
-        def _():
-            fetch(x_far, x, arrived, step + 1).wait()
+        for n in range(STEP // PIECE):
+            piece = step * (STEP // PIECE) + n + 1
+
+            @pl.when(piece + AHEAD - 1 < pieces)
+            def _():
+                fetch(x_far, x, arrived, piece + AHEAD - 1).start()
+
+            @pl.when(piece < pieces)
+            def _():
+                fetch(x_far, x, arrived, piece).wait()
 
         first = step * STEP
         for n in range(STEP):
@@ -157,7 +161,7 @@
             reduce(first + n, *here)
         return carry
 
-    lax.fori_loop(0, pieces, several, 0)
+    lax.fori_loop(0, chunks // STEP, several, 0)
 
     scaled = []
     top = jnp.zeros((1, 1), F32)
@@ -270,8 +274,9 @@
     )(names, place, near(table))
     chosen = lax.all_to_all(chosen, "rep", 0, 0, tiled=True)
 
-    gram = summed(gram, "blk_1", (1, 2))
     gram = summed(gram, "blk_0", (4,))
+    gram = summed(gram, "blk_0", (2,))
+    gram = summed(gram, "blk_0", (1,))
 
     parts = pl.pallas_call(
         contract_kernel,
@@ -280,7 +285,7 @@
         out_specs=whole(),
         scratch_shapes=[
             VMEM((slots, BS, BS, BS), BF16),
-            pltpu.SemaphoreType.DMA((slots * BS // (STEP * CHUNK),)),
+            pltpu.SemaphoreType.DMA((slots * BS // (PIECE * CHUNK),)),
             VMEM((slots, 2, BS, rank), F32),
             VMEM((slots, BS, rank), BF16),
             VMEM((slots, BS, rank), BF16),
@@ -302,7 +307,8 @@
     )
     parts = lax.all_to_all(parts.astype(F16), "rep", 0, 0, tiled=True)
 
-    gram = summed(gram, "blk_0", (1, 2))
+    gram = summed(gram, "blk_1", (1,))
+    gram = summed(gram, "blk_1", (2,))
     fitted = pl.pallas_call(
         fit_kernel,
         out_shape=jax.ShapeDtypeStruct((per_owner, width, BS), F32),

time: 108 us -> 118 us (1.093)
  waiting for transfers between devices: 36.3 us -> 50.1 us
  starting transfers between devices: 37.8 us -> 34.1 us
    ppermute x8, waiting for transfers between devices: 22.7 us -> 36.4 us  [swapped(): return lax.ppermute(array, axis, [(i, i ^ bit) for i in range(peers)])]
    ppermute x8, starting transfers between devices: 16.2 us -> 12.5 us  [swapped(): return lax.ppermute(array, axis, [(i, i ^ bit) for i in range(peers)])]
where the time goes in v3:
time: 118 us; the launch traced here: 117 us
  waiting for transfers between devices  50.1 us (42%)
  starting transfers between devices  34.1 us (29%)
  Pallas kernels  16.7 us (14%)
  blocking collectives  11.5 us (10%)
  other arithmetic  2.25 us (2%)
  local copies, waits for them, and re-layouts  1.73 us (1%)
    ppermute x8, waiting for transfers between devices, swapped(): return lax.ppermute(array, axis, [(i, i ^ bit) for i in range(peers)])  36.4 us
    pallas_call x1, Pallas kernels, shards(): pl.pallas_call(contract_kernel, out_shape=VMEM((reps, named * width + SUB...  13.9 us
    ppermute x8, starting transfers between devices, swapped(): return lax.ppermute(array, axis, [(i, i ^ bit) for i in range(peers)])  12.5 us
    all_to_all x1, starting transfers between devices, shards(): lax.all_to_all(jnp.broadcast_to(own[None], (owners, *own.shape)), BLK, 0,...  11.7 us
    all_to_all x1, blocking collectives, shards(): parts = lax.all_to_all(parts.astype(F16), 'rep', 0, 0, tiled=True)  11.5 us
    all_to_all x1, waiting for transfers between devices, shards(): chosen = lax.all_to_all(chosen, 'rep', 0, 0, tiled=True)  8.26 us
    all_to_all x1, starting transfers between devices, shards(): arrived = lax.all_to_all(scaled.astype(F16), BLK, 0, 0, tiled=True)  5.57 us
    all_to_all x1, waiting for transfers between devices, shards(): lax.all_to_all(jnp.broadcast_to(own[None], (owners, *own.shape)), BLK, 0,...  5.4 us
  transfers between devices with their start and end apart: 11, of which 10 were waited for; matrix products, arithmetic and copies ran while one was open for 0% of the time, Pallas kernels for 0%

profile of v3, /device:TPU:8, one launch (start us, length us, event | category | flops | bytes accessed | tf_op | source)
XLA Modules:
  0.0 117.1 jit_solution(8416112585798408606)
XLA Ops:
  0.0 0.0 copy-start
  0.0 0.0 copy-start.1
  0.0 0.7 copy-done
  0.7 0.9 broadcast_in_dim.10
  1.6 11.7 %all-to-all-start = ((bf16[32,2,32,128]{3,2,1,0:T(8,128)(2,1)}), bf16[32,2,32,128]{3,2,1,0:T(8,128)(2,1)S(1)}, u32[]{:S(2)}, u32[]{:S(2)}) async-start(bf16[32,2,32,128]{3,2,1,0:T(8,128)(2,1)} %broadcast_in_dim.10), calls=%async_computation | async-start | bytes 1048576 | tf_op jit(solution)/shard_map/all_to_all | solution.py:250
  13.3 0.0 copy-done.1
  13.4 0.1 convert_element_type.34
  13.5 0.1 collective-permute-start
  13.5 1.2 %collective-permute-done = bf16[1,80,128]{2,1,0:T(8,128)(2,1)S(1)} collective-permute-done((bf16[1,80,128]{2,1,0:T(8,128)(2,1)S(1)}, bf16[1,80,128]{2,1,0:T(8,128)(2,1)S(1)}, u32[]{:S(2)}, u32[]{:S(2)}) %collective-permute-start) | collective-permute-done | bytes 20512 | tf_op jit(solution)/shard_map/ppermute | solution.py:223
  14.7 1.5 %collective-permute-start.1 = (bf16[2,80,128]{2,1,0:T(8,128)(2,1)S(1)}, bf16[2,80,128]{2,1,0:T(8,128)(2,1)S(1)}, u32[]{:S(2)}, u32[]{:S(2)}) collective-permute-start(bf16[2,80,128]{2,1,0:T(8,128)(2,1)S(1)} %pad_maximum_fusion.2), channel_id=1, source_target_pairs={{0,2},{1,3},{2,0},{3,1},{4,6},{5,7},{6,4},{7,5},{8,10},{9,11},{10,... | collective-permute-start | bytes 122888 | tf_op jit(solution)/shard_map/ppermute | solution.py:223
  16.2 2.5 %collective-permute-done.1 = bf16[2,80,128]{2,1,0:T(8,128)(2,1)S(1)} collective-permute-done((bf16[2,80,128]{2,1,0:T(8,128)(2,1)S(1)}, bf16[2,80,128]{2,1,0:T(8,128)(2,1)S(1)}, u32[]{:S(2)}, u32[]{:S(2)}) %collective-permute-start.1) | collective-permute-done | bytes 40992 | tf_op jit(solution)/shard_map/ppermute | solution.py:223
  18.7 3.1 %collective-permute-start.2 = (bf16[4,80,128]{2,1,0:T(8,128)(2,1)S(1)}, bf16[4,80,128]{2,1,0:T(8,128)(2,1)S(1)}, u32[]{:S(2)}, u32[]{:S(2)}) collective-permute-start(bf16[4,80,128]{2,1,0:T(8,128)(2,1)S(1)} %pad_maximum_fusion.1), channel_id=1, source_target_pairs={{0,4},{1,5},{2,6},{3,7},{4,0},{5,1},{6,2},{7,3},{8,12},{9,13},{10,... | collective-permute-start | bytes 245768 | tf_op jit(solution)/shard_map/ppermute | solution.py:223
  21.8 2.9 %collective-permute-done.2 = bf16[4,80,128]{2,1,0:T(8,128)(2,1)S(1)} collective-permute-done((bf16[4,80,128]{2,1,0:T(8,128)(2,1)S(1)}, bf16[4,80,128]{2,1,0:T(8,128)(2,1)S(1)}, u32[]{:S(2)}, u32[]{:S(2)}) %collective-permute-start.2) | collective-permute-done | bytes 81952 | tf_op jit(solution)/shard_map/ppermute | solution.py:223
  24.8 5.4 %all-to-all-done = bf16[32,2,32,128]{3,2,1,0:T(8,128)(2,1)S(1)} async-done(((bf16[32,2,32,128]{3,2,1,0:T(8,128)(2,1)}), bf16[32,2,32,128]{3,2,1,0:T(8,128)(2,1)S(1)}, u32[]{:S(2)}, u32[]{:S(2)}) %all-to-all-start) | async-done | bytes 524320 | tf_op jit(solution)/shard_map/all_to_all | solution.py:250
  30.2 1.4 %select.8 = bf16[8,6,32,128]{3,2,1,0:T(8,128)(2,1)} custom-call(s32[8,6]{1,0:T(8,128)S(1)} %bitcast.30, s32[1]{0:T(128)} %bitcast.6.place, bf16[64,32,128]{2,1,0:T(8,128)(2,1)S(1)} %bitcast.27), custom_call_target="tpu_custom_call" | custom-call | tf_op jit(solution)/shard_map/select/pallas_call | solution.py:267
  31.6 4.3 %all-to-all-start.1 = ((bf16[8,6,32,128]{3,2,1,0:T(8,128)(2,1)}), bf16[8,6,32,128]{3,2,1,0:T(8,128)(2,1)S(1)}, u32[]{:S(2)}, u32[]{:S(2)}) async-start(bf16[8,6,32,128]{3,2,1,0:T(8,128)(2,1)} %select.8), calls=%async_computation.1 | async-start | bytes 786432 | tf_op jit(solution)/shard_map/all_to_all | solution.py:275
  36.5 8.3 %all-to-all-done.1.sel = bf16[8,6,32,128]{3,2,1,0:T(8,128)(2,1)S(1)} async-done(((bf16[8,6,32,128]{3,2,1,0:T(8,128)(2,1)}), bf16[8,6,32,128]{3,2,1,0:T(8,128)(2,1)S(1)}, u32[]{:S(2)}, u32[]{:S(2)}) %all-to-all-start.1) | async-done | bytes 393248 | tf_op jit(solution)/shard_map/all_to_all | solution.py:275
  44.8 13.9 %contract.1 = f32[8,200,128]{2,1,0:T(8,128)S(1)} custom-call(s32[2,3]{1,0:T(2,128)S(1)} %copy-done.1, s32[1]{0:T(128)S(6)} %copy.15.count, bf16[2,128,128,128]{3,2,1,0:T(8,128)(2,1)} %x_far.1, bf16[8,6,32,128]{3,2,1,0:T(8,128)(2,1)S(1)} %all-to-all-done.1.sel), custom_call_target="tpu_custom_call" | custom-call | tf_op jit(solution)/shard_map/contract/pallas_call | solution.py:281
  58.7 0.1 convert_element_type.37
  58.8 11.5 %all_to_all.20 = f16[8,200,128]{2,1,0:T(8,128)(2,1)S(1)} all-to-all(f16[8,200,128]{2,1,0:T(8,128)(2,1)S(1)} %convert_element_type.37), channel_id=1, replica_groups=mesh['blk_0'=8,'blk_1'=4,'rep'=8] {'rep'}, dimensions={0} | all-to-all | bytes 819200 | tf_op jit(solution)/shard_map/all_to_all | solution.py:308
  70.3 0.1 convert_element_type.38.parts
  70.3 1.1 scatter.1
  71.4 0.9 convert_element_type.39
  72.3 5.6 %all-to-all-start.3 = ((f16[32,72,128]{2,1,0:T(8,128)(2,1)}), f16[32,72,128]{2,1,0:T(8,128)(2,1)S(1)}, u32[]{:S(2)}, u32[]{:S(2)}) async-start(f16[32,72,128]{2,1,0:T(8,128)(2,1)} %convert_element_type.39), calls=%async_computation.3 | async-start | bytes 1179648 | tf_op jit(solution)/shard_map/all_to_all | solution.py:331
  77.9 0.1 gram.1
  78.1 5.4 %collective-permute-start.3 = (f32[32,256]{1,0:T(8,128)S(1)}, f32[32,256]{1,0:T(8,128)S(1)}, u32[]{:S(2)}, u32[]{:S(2)}) collective-permute-start(f32[32,256]{1,0:T(8,128)S(1)} %gram.1), channel_id=1, source_target_pairs={{0,128},{32,160},{64,192},{96,224},{128,0},{160,32},{192,64},{224,... | collective-permute-start | bytes 98312 | tf_op jit(solution)/shard_map/ppermute | solution.py:223
  83.5 13.8 %collective-permute-done.3 = f32[32,256]{1,0:T(8,128)S(1)} collective-permute-done((f32[32,256]{1,0:T(8,128)S(1)}, f32[32,256]{1,0:T(8,128)S(1)}, u32[]{:S(2)}, u32[]{:S(2)}) %collective-permute-start.3) | collective-permute-done | bytes 32800 | tf_op jit(solution)/shard_map/ppermute | solution.py:223
  97.3 0.0 collective-permute-start.4
  97.3 5.2 %collective-permute-done.4 = f32[32,256]{1,0:T(8,128)S(1)} collective-permute-done((f32[32,256]{1,0:T(8,128)S(1)}, f32[32,256]{1,0:T(8,128)S(1)}, u32[]{:S(2)}, u32[]{:S(2)}) %collective-permute-start.4) | collective-permute-done | bytes 32800 | tf_op jit(solution)/shard_map/ppermute | solution.py:223
  102.5 0.3 collective-permute-start.5
  102.8 3.6 %collective-permute-done.5 = f32[32,256]{1,0:T(8,128)S(1)} collective-permute-done((f32[32,256]{1,0:T(8,128)S(1)}, f32[32,256]{1,0:T(8,128)S(1)}, u32[]{:S(2)}, u32[]{:S(2)}) %collective-permute-start.5) | collective-permute-done | bytes 32800 | tf_op jit(solution)/shard_map/ppermute | solution.py:223
  106.4 0.0 collective-permute-start.6
  106.4 3.9 %collective-permute-done.6 = f32[32,256]{1,0:T(8,128)S(1)} collective-permute-done((f32[32,256]{1,0:T(8,128)S(1)}, f32[32,256]{1,0:T(8,128)S(1)}, u32[]{:S(2)}, u32[]{:S(2)}) %collective-permute-start.6) | collective-permute-done | bytes 32800 | tf_op jit(solution)/shard_map/ppermute | solution.py:223
  110.3 2.1 %collective-permute-start.7 = (f32[32,256]{1,0:T(8,128)S(1)}, f32[32,256]{1,0:T(8,128)S(1)}, u32[]{:S(2)}, u32[]{:S(2)}) collective-permute-start(f32[32,256]{1,0:T(8,128)S(1)} %add.20), channel_id=1, source_target_pairs={{0,16},{8,24},{16,0},{24,8},{1,17},{9,25},{17,1},{25,9},{2,18},{10... | collective-permute-start | bytes 98312 | tf_op jit(solution)/shard_map/ppermute | solution.py:223
  112.4 3.3 %collective-permute-done.7 = f32[32,256]{1,0:T(8,128)S(1)} collective-permute-done((f32[32,256]{1,0:T(8,128)S(1)}, f32[32,256]{1,0:T(8,128)S(1)}, u32[]{:S(2)}, u32[]{:S(2)}) %collective-permute-start.7) | collective-permute-done | bytes 32800 | tf_op jit(solution)/shard_map/ppermute | solution.py:223
  115.8 0.2 fit.1
  115.9 0.0 all-to-all-done.3
  116.0 0.1 convert_element_type.40
  116.0 0.3 fusion.6
  116.4 0.1 fusion
  116.5 0.6 bitcast_bitcast_fusion
  (13 shorter events, 0.1 us)
Async XLA Ops:
  0.0 0.7 copy-start
  0.0 13.3 %copy-start.1 = (s32[2,3]{1,0:T(2,128)S(1)}, s32[2,3]{1,0:T(2,128)}, u32[]{:S(2)}) copy-start(s32[2,3]{1,0:T(2,128)} %triples.1) | copy-start | bytes 76
  1.6 28.5 %all-to-all-start = ((bf16[32,2,32,128]{3,2,1,0:T(8,128)(2,1)}), bf16[32,2,32,128]{3,2,1,0:T(8,128)(2,1)S(1)}, u32[]{:S(2)}, u32[]{:S(2)}) async-start(bf16[32,2,32,128]{3,2,1,0:T(8,128)(2,1)} %broadcast_in_dim.10), calls=%async_computation | async-start | bytes 1048576 | tf_op jit(solution)/shard_map/all_to_all | solution.py:250
  13.5 1.2 %collective-permute-start = (bf16[1,80,128]{2,1,0:T(8,128)(2,1)S(1)}, bf16[1,80,128]{2,1,0:T(8,128)(2,1)S(1)}, u32[]{:S(2)}, u32[]{:S(2)}) collective-permute-start(bf16[1,80,128]{2,1,0:T(8,128)(2,1)S(1)} %fusion.3), channel_id=1, source_target_pairs={{0,1},{1,0},{2,3},{3,2},{4,5},{5,4},{6,7},{7,6},{8,9},{9,8},{10,11... | collective-permute-start | bytes 61448 | tf_op jit(solution)/shard_map/ppermute | solution.py:223
  14.7 4.0 %collective-permute-start.1 = (bf16[2,80,128]{2,1,0:T(8,128)(2,1)S(1)}, bf16[2,80,128]{2,1,0:T(8,128)(2,1)S(1)}, u32[]{:S(2)}, u32[]{:S(2)}) collective-permute-start(bf16[2,80,128]{2,1,0:T(8,128)(2,1)S(1)} %pad_maximum_fusion.2), channel_id=1, source_target_pairs={{0,2},{1,3},{2,0},{3,1},{4,6},{5,7},{6,4},{7,5},{8,10},{9,11},{10,... | collective-permute-start | bytes 122888 | tf_op jit(solution)/shard_map/ppermute | solution.py:223
  18.7 6.0 %collective-permute-start.2 = (bf16[4,80,128]{2,1,0:T(8,128)(2,1)S(1)}, bf16[4,80,128]{2,1,0:T(8,128)(2,1)S(1)}, u32[]{:S(2)}, u32[]{:S(2)}) collective-permute-start(bf16[4,80,128]{2,1,0:T(8,128)(2,1)S(1)} %pad_maximum_fusion.1), channel_id=1, source_target_pairs={{0,4},{1,5},{2,6},{3,7},{4,0},{5,1},{6,2},{7,3},{8,12},{9,13},{10,... | collective-permute-start | bytes 245768 | tf_op jit(solution)/shard_map/ppermute | solution.py:223
  31.6 13.2 %all-to-all-start.1 = ((bf16[8,6,32,128]{3,2,1,0:T(8,128)(2,1)}), bf16[8,6,32,128]{3,2,1,0:T(8,128)(2,1)S(1)}, u32[]{:S(2)}, u32[]{:S(2)}) async-start(bf16[8,6,32,128]{3,2,1,0:T(8,128)(2,1)} %select.8), calls=%async_computation.1 | async-start | bytes 786432 | tf_op jit(solution)/shard_map/all_to_all | solution.py:275
  72.3 43.6 %all-to-all-start.3 = ((f16[32,72,128]{2,1,0:T(8,128)(2,1)}), f16[32,72,128]{2,1,0:T(8,128)(2,1)S(1)}, u32[]{:S(2)}, u32[]{:S(2)}) async-start(f16[32,72,128]{2,1,0:T(8,128)(2,1)} %convert_element_type.39), calls=%async_computation.3 | async-start | bytes 1179648 | tf_op jit(solution)/shard_map/all_to_all | solution.py:331
  78.1 19.2 %collective-permute-start.3 = (f32[32,256]{1,0:T(8,128)S(1)}, f32[32,256]{1,0:T(8,128)S(1)}, u32[]{:S(2)}, u32[]{:S(2)}) collective-permute-start(f32[32,256]{1,0:T(8,128)S(1)} %gram.1), channel_id=1, source_target_pairs={{0,128},{32,160},{64,192},{96,224},{128,0},{160,32},{192,64},{224,... | collective-permute-start | bytes 98312 | tf_op jit(solution)/shard_map/ppermute | solution.py:223
  97.3 5.2 %collective-permute-start.4 = (f32[32,256]{1,0:T(8,128)S(1)}, f32[32,256]{1,0:T(8,128)S(1)}, u32[]{:S(2)}, u32[]{:S(2)}) collective-permute-start(f32[32,256]{1,0:T(8,128)S(1)} %add.17), channel_id=1, source_target_pairs={{0,64},{32,96},{64,0},{96,32},{128,192},{160,224},{192,128},{224,1... | collective-permute-start | bytes 98312 | tf_op jit(solution)/shard_map/ppermute | solution.py:223
  102.5 3.9 %collective-permute-start.5 = (f32[32,256]{1,0:T(8,128)S(1)}, f32[32,256]{1,0:T(8,128)S(1)}, u32[]{:S(2)}, u32[]{:S(2)}) collective-permute-start(f32[32,256]{1,0:T(8,128)S(1)} %add.18), channel_id=1, source_target_pairs={{0,32},{32,0},{64,96},{96,64},{128,160},{160,128},{192,224},{224,1... | collective-permute-start | bytes 98312 | tf_op jit(solution)/shard_map/ppermute | solution.py:223
  106.4 3.9 %collective-permute-start.6 = (f32[32,256]{1,0:T(8,128)S(1)}, f32[32,256]{1,0:T(8,128)S(1)}, u32[]{:S(2)}, u32[]{:S(2)}) collective-permute-start(f32[32,256]{1,0:T(8,128)S(1)} %add.19), channel_id=1, source_target_pairs={{0,8},{8,0},{16,24},{24,16},{1,9},{9,1},{17,25},{25,17},{2,10},{10... | collective-permute-start | bytes 98312 | tf_op jit(solution)/shard_map/ppermute | solution.py:223
  110.3 5.4 %collective-permute-start.7 = (f32[32,256]{1,0:T(8,128)S(1)}, f32[32,256]{1,0:T(8,128)S(1)}, u32[]{:S(2)}, u32[]{:S(2)}) collective-permute-start(f32[32,256]{1,0:T(8,128)S(1)} %add.20), channel_id=1, source_target_pairs={{0,16},{8,24},{16,0},{24,8},{1,17},{9,25},{17,1},{25,9},{2,18},{10... | collective-permute-start | bytes 98312 | tf_op jit(solution)/shard_map/ppermute | solution.py:223

commit v4 on v3

--- a/solution.py
+++ b/solution.py
@@ -15,6 +15,7 @@
 SUBLANES = 8
 STEP = 8
 PIECE = 4
+GROUP = 2
 AHEAD = 3
 F32 = jnp.float32
 BF16 = jnp.bfloat16
@@ -77,7 +78,7 @@
 
 def contract_kernel(
     triples, count, x_far, sel, out,
-    x, arrived, fac, low, mid, lower_a, middle_a, lower_b, middle_b, y1, y2, y3,
+    x, arrived, fac, low, mid, y1, y2, y3,
 ):
     slots = x.shape[0]
     reps, _, width, _ = sel.shape
@@ -99,66 +100,53 @@
     y2[...] = jnp.zeros_like(y2)
     y3[...] = jnp.zeros_like(y3)
 
-    def multiply(chunk, lower_s, middle_s):
-        slot = chunk // per_slot
-        row0 = pl.multiple_of(lax.rem(chunk, per_slot) * CHUNK, CHUNK)
-        blocks = x[slot, pl.ds(row0, CHUNK)]
-        lower_s[...] = jnp.dot(
-            blocks.reshape(CHUNK * BS, BS), low[slot], preferred_element_type=F32
-        ).reshape(CHUNK, BS, rank)
-        turned = jnp.concatenate([blocks[a].T for a in range(CHUNK)], axis=0)
-        middle_s[...] = jnp.dot(turned, mid[slot], preferred_element_type=F32).reshape(
-            CHUNK, BS, rank
-        )
-
-    def reduce(chunk, lower_s, middle_s):
-        slot = chunk // per_slot
-        row0 = pl.multiple_of(lax.rem(chunk, per_slot) * CHUNK, CHUNK)
-        for half in range(rank // BS):
-            cols = slice(half * BS, (half + 1) * BS)
-            upper_rows = fac[slot, 0, pl.ds(row0, CHUNK), cols]
-            spread = [
-                jnp.broadcast_to(upper_rows[a : a + 1], (SUBLANES, BS)) for a in range(CHUNK)
-            ]
-            sums = [jnp.zeros((SUBLANES, BS), F32) for _ in range(CHUNK)]
-            for b in range(0, BS, SUBLANES):
-                rows = slice(b, b + SUBLANES)
-                other = fac[slot, 1, rows, cols]
-                second = y2[slot, rows, cols]
-                third = y3[slot, rows, cols]
-                for a in range(CHUNK):
-                    value = lower_s[a, rows, cols]
-                    sums[a] = sums[a] + value * other
-                    second = second + value * spread[a]
-                    third = third + middle_s[a, rows, cols] * spread[a]
-                y2[slot, rows, cols] = second
-                y3[slot, rows, cols] = third
-            y1[slot, pl.ds(row0, CHUNK), cols] = jnp.concatenate(
-                [jnp.sum(sums[a], axis=0, keepdims=True) for a in range(CHUNK)], axis=0
-            )
-
-    fetch(x_far, x, arrived, 0).wait()
-    multiply(0, lower_a, middle_a)
-
     def several(step, carry):
         for n in range(STEP // PIECE):
-            piece = step * (STEP // PIECE) + n + 1
-
-            @pl.when(piece + AHEAD - 1 < pieces)
+            piece = step * (STEP // PIECE) + n
+
+            @pl.when(piece + AHEAD < pieces)
             def _():
-                fetch(x_far, x, arrived, piece + AHEAD - 1).start()
-
-            @pl.when(piece < pieces)
-            def _():
-                fetch(x_far, x, arrived, piece).wait()
-
-        first = step * STEP
+                fetch(x_far, x, arrived, piece + AHEAD).start()
+
+            fetch(x_far, x, arrived, piece).wait()
         for n in range(STEP):
-            here, there = (lower_a, middle_a), (lower_b, middle_b)
-            if n % 2:
-                here, there = there, here
-            multiply(jnp.minimum(first + n + 1, chunks - 1), *there)
-            reduce(first + n, *here)
+            chunk = step * STEP + n
+            slot = chunk // per_slot
+            row0 = pl.multiple_of(lax.rem(chunk, per_slot) * CHUNK, CHUNK)
+            lower = low[slot]
+            middle = mid[slot]
+            firsts = [[] for _ in range(rank // BS)]
+            for a0 in range(0, CHUNK, GROUP):
+                blocks = x[slot, pl.ds(row0 + a0, GROUP)]
+                ls = jnp.dot(
+                    blocks.reshape(GROUP * BS, BS), lower, preferred_element_type=F32
+                ).reshape(GROUP, BS, rank)
+                turned = jnp.concatenate([blocks[a].T for a in range(GROUP)], axis=0)
+                ms = jnp.dot(turned, middle, preferred_element_type=F32).reshape(GROUP, BS, rank)
+                upper = fac[slot, 0, pl.ds(row0, CHUNK)]
+                for half in range(rank // BS):
+                    cols = slice(half * BS, (half + 1) * BS)
+                    spread = [
+                        jnp.broadcast_to(upper[a0 + a : a0 + a + 1, cols], (SUBLANES, BS))
+                        for a in range(GROUP)
+                    ]
+                    sums = [jnp.zeros((SUBLANES, BS), F32) for _ in range(GROUP)]
+                    for b in range(0, BS, SUBLANES):
+                        rows = slice(b, b + SUBLANES)
+                        other = fac[slot, 1, rows, cols]
+                        second = y2[slot, rows, cols]
+                        third = y3[slot, rows, cols]
+                        for a in range(GROUP):
+                            value = ls[a, rows, cols]
+                            sums[a] = sums[a] + value * other
+                            second = second + value * spread[a]
+                            third = third + ms[a, rows, cols] * spread[a]
+                        y2[slot, rows, cols] = second
+                        y3[slot, rows, cols] = third
+                    firsts[half].extend(jnp.sum(v, axis=0, keepdims=True) for v in sums)
+            for half in range(rank // BS):
+                cols = slice(half * BS, (half + 1) * BS)
+                y1[slot, pl.ds(row0, CHUNK), cols] = jnp.concatenate(firsts[half], axis=0)
         return carry
 
     lax.fori_loop(0, chunks // STEP, several, 0)
@@ -289,10 +277,6 @@
             VMEM((slots, 2, BS, rank), F32),
             VMEM((slots, BS, rank), BF16),
             VMEM((slots, BS, rank), BF16),
-            VMEM((CHUNK, BS, rank), F32),
-            VMEM((CHUNK, BS, rank), F32),
-            VMEM((CHUNK, BS, rank), F32),
-            VMEM((CHUNK, BS, rank), F32),
             VMEM((slots, BS, rank), F32),
             VMEM((slots, BS, rank), F32),
             VMEM((slots, BS, rank), F32),

time: 118 us -> 116 us (0.983)
  Pallas kernels: 16.7 us -> 15 us
    pallas_call x1, Pallas kernels: 13.9 us -> 12.2 us  [shards(): pl.pallas_call(contract_kernel, out_shape=VMEM((reps, named * width + SUB...]
where the time goes in v4:
time: 116 us; the launch traced here: 115 us
  waiting for transfers between devices  50.1 us (43%)
  starting transfers between devices  34.1 us (29%)
  Pallas kernels  15 us (13%)
  blocking collectives  11.5 us (10%)
  other arithmetic  2.25 us (2%)
  local copies, waits for them, and re-layouts  1.73 us (1%)
    ppermute x8, waiting for transfers between devices, swapped(): return lax.ppermute(array, axis, [(i, i ^ bit) for i in range(peers)])  36.4 us
    ppermute x8, starting transfers between devices, swapped(): return lax.ppermute(array, axis, [(i, i ^ bit) for i in range(peers)])  12.5 us
    pallas_call x1, Pallas kernels, shards(): pl.pallas_call(contract_kernel, out_shape=VMEM((reps, named * width + SUB...  12.2 us
    all_to_all x1, starting transfers between devices, shards(): lax.all_to_all(jnp.broadcast_to(own[None], (owners, *own.shape)), BLK, 0,...  11.7 us
    all_to_all x1, blocking collectives, shards(): parts = lax.all_to_all(parts.astype(F16), 'rep', 0, 0, tiled=True)  11.5 us
    all_to_all x1, waiting for transfers between devices, shards(): chosen = lax.all_to_all(chosen, 'rep', 0, 0, tiled=True)  8.26 us
    all_to_all x1, starting transfers between devices, shards(): arrived = lax.all_to_all(scaled.astype(F16), BLK, 0, 0, tiled=True)  5.57 us
    all_to_all x1, waiting for transfers between devices, shards(): lax.all_to_all(jnp.broadcast_to(own[None], (owners, *own.shape)), BLK, 0,...  5.4 us
  transfers between devices with their start and end apart: 11, of which 10 were waited for; matrix products, arithmetic and copies ran while one was open for 0% of the time, Pallas kernels for 0%

profile of v4, /device:TPU:8, one launch (start us, length us, event | category | flops | bytes accessed | tf_op | source)
XLA Modules:
  0.0 115.4 jit_solution(12137479969261015357)
XLA Ops:
  0.0 0.0 copy-start
  0.0 0.0 copy-start.1
  0.0 0.7 copy-done
  0.7 0.9 broadcast_in_dim.10
  1.6 11.7 %all-to-all-start = ((bf16[32,2,32,128]{3,2,1,0:T(8,128)(2,1)}), bf16[32,2,32,128]{3,2,1,0:T(8,128)(2,1)S(1)}, u32[]{:S(2)}, u32[]{:S(2)}) async-start(bf16[32,2,32,128]{3,2,1,0:T(8,128)(2,1)} %broadcast_in_dim.10), calls=%async_computation | async-start | bytes 1048576 | tf_op jit(solution)/shard_map/all_to_all | solution.py:238
  13.3 0.0 copy-done.1
  13.4 0.1 convert_element_type.34
  13.5 0.1 collective-permute-start
  13.5 1.2 %collective-permute-done = bf16[1,80,128]{2,1,0:T(8,128)(2,1)S(1)} collective-permute-done((bf16[1,80,128]{2,1,0:T(8,128)(2,1)S(1)}, bf16[1,80,128]{2,1,0:T(8,128)(2,1)S(1)}, u32[]{:S(2)}, u32[]{:S(2)}) %collective-permute-start) | collective-permute-done | bytes 20512 | tf_op jit(solution)/shard_map/ppermute | solution.py:211
  14.7 1.5 %collective-permute-start.1 = (bf16[2,80,128]{2,1,0:T(8,128)(2,1)S(1)}, bf16[2,80,128]{2,1,0:T(8,128)(2,1)S(1)}, u32[]{:S(2)}, u32[]{:S(2)}) collective-permute-start(bf16[2,80,128]{2,1,0:T(8,128)(2,1)S(1)} %pad_maximum_fusion.2), channel_id=1, source_target_pairs={{0,2},{1,3},{2,0},{3,1},{4,6},{5,7},{6,4},{7,5},{8,10},{9,11},{10,... | collective-permute-start | bytes 122888 | tf_op jit(solution)/shard_map/ppermute | solution.py:211
  16.2 2.5 %collective-permute-done.1 = bf16[2,80,128]{2,1,0:T(8,128)(2,1)S(1)} collective-permute-done((bf16[2,80,128]{2,1,0:T(8,128)(2,1)S(1)}, bf16[2,80,128]{2,1,0:T(8,128)(2,1)S(1)}, u32[]{:S(2)}, u32[]{:S(2)}) %collective-permute-start.1) | collective-permute-done | bytes 40992 | tf_op jit(solution)/shard_map/ppermute | solution.py:211
  18.7 3.1 %collective-permute-start.2 = (bf16[4,80,128]{2,1,0:T(8,128)(2,1)S(1)}, bf16[4,80,128]{2,1,0:T(8,128)(2,1)S(1)}, u32[]{:S(2)}, u32[]{:S(2)}) collective-permute-start(bf16[4,80,128]{2,1,0:T(8,128)(2,1)S(1)} %pad_maximum_fusion.1), channel_id=1, source_target_pairs={{0,4},{1,5},{2,6},{3,7},{4,0},{5,1},{6,2},{7,3},{8,12},{9,13},{10,... | collective-permute-start | bytes 245768 | tf_op jit(solution)/shard_map/ppermute | solution.py:211
  21.8 2.9 %collective-permute-done.2 = bf16[4,80,128]{2,1,0:T(8,128)(2,1)S(1)} collective-permute-done((bf16[4,80,128]{2,1,0:T(8,128)(2,1)S(1)}, bf16[4,80,128]{2,1,0:T(8,128)(2,1)S(1)}, u32[]{:S(2)}, u32[]{:S(2)}) %collective-permute-start.2) | collective-permute-done | bytes 81952 | tf_op jit(solution)/shard_map/ppermute | solution.py:211
  24.8 5.4 %all-to-all-done = bf16[32,2,32,128]{3,2,1,0:T(8,128)(2,1)S(1)} async-done(((bf16[32,2,32,128]{3,2,1,0:T(8,128)(2,1)}), bf16[32,2,32,128]{3,2,1,0:T(8,128)(2,1)S(1)}, u32[]{:S(2)}, u32[]{:S(2)}) %all-to-all-start) | async-done | bytes 524320 | tf_op jit(solution)/shard_map/all_to_all | solution.py:238
  30.2 1.4 %select.8 = bf16[8,6,32,128]{3,2,1,0:T(8,128)(2,1)} custom-call(s32[8,6]{1,0:T(8,128)S(1)} %bitcast.30, s32[1]{0:T(128)} %bitcast.6.place, bf16[64,32,128]{2,1,0:T(8,128)(2,1)S(1)} %bitcast.27), custom_call_target="tpu_custom_call" | custom-call | tf_op jit(solution)/shard_map/select/pallas_call | solution.py:255
  31.6 4.3 %all-to-all-start.1 = ((bf16[8,6,32,128]{3,2,1,0:T(8,128)(2,1)}), bf16[8,6,32,128]{3,2,1,0:T(8,128)(2,1)S(1)}, u32[]{:S(2)}, u32[]{:S(2)}) async-start(bf16[8,6,32,128]{3,2,1,0:T(8,128)(2,1)} %select.8), calls=%async_computation.1 | async-start | bytes 786432 | tf_op jit(solution)/shard_map/all_to_all | solution.py:263
  36.5 8.3 %all-to-all-done.1.sel = bf16[8,6,32,128]{3,2,1,0:T(8,128)(2,1)S(1)} async-done(((bf16[8,6,32,128]{3,2,1,0:T(8,128)(2,1)}), bf16[8,6,32,128]{3,2,1,0:T(8,128)(2,1)S(1)}, u32[]{:S(2)}, u32[]{:S(2)}) %all-to-all-start.1) | async-done | bytes 393248 | tf_op jit(solution)/shard_map/all_to_all | solution.py:263
  44.8 12.2 %contract.1 = f32[8,200,128]{2,1,0:T(8,128)S(1)} custom-call(s32[2,3]{1,0:T(2,128)S(1)} %copy-done.1, s32[1]{0:T(128)S(6)} %copy.15.count, bf16[2,128,128,128]{3,2,1,0:T(8,128)(2,1)} %x_far.1, bf16[8,6,32,128]{3,2,1,0:T(8,128)(2,1)S(1)} %all-to-all-done.1.sel), custom_call_target="tpu_custom_call" | custom-call | tf_op jit(solution)/shard_map/contract/pallas_call | solution.py:269
  57.0 0.1 convert_element_type.37
  57.1 11.5 %all_to_all.20 = f16[8,200,128]{2,1,0:T(8,128)(2,1)S(1)} all-to-all(f16[8,200,128]{2,1,0:T(8,128)(2,1)S(1)} %convert_element_type.37), channel_id=1, replica_groups=mesh['blk_0'=8,'blk_1'=4,'rep'=8] {'rep'}, dimensions={0} | all-to-all | bytes 819200 | tf_op jit(solution)/shard_map/all_to_all | solution.py:292
  68.6 0.1 convert_element_type.38.parts
  68.6 1.1 scatter.1
  69.7 0.9 convert_element_type.39
  70.6 5.6 %all-to-all-start.3 = ((f16[32,72,128]{2,1,0:T(8,128)(2,1)}), f16[32,72,128]{2,1,0:T(8,128)(2,1)S(1)}, u32[]{:S(2)}, u32[]{:S(2)}) async-start(f16[32,72,128]{2,1,0:T(8,128)(2,1)} %convert_element_type.39), calls=%async_computation.3 | async-start | bytes 1179648 | tf_op jit(solution)/shard_map/all_to_all | solution.py:315
  76.2 0.1 gram.1
  76.4 5.4 %collective-permute-start.3 = (f32[32,256]{1,0:T(8,128)S(1)}, f32[32,256]{1,0:T(8,128)S(1)}, u32[]{:S(2)}, u32[]{:S(2)}) collective-permute-start(f32[32,256]{1,0:T(8,128)S(1)} %gram.1), channel_id=1, source_target_pairs={{0,128},{32,160},{64,192},{96,224},{128,0},{160,32},{192,64},{224,... | collective-permute-start | bytes 98312 | tf_op jit(solution)/shard_map/ppermute | solution.py:211
  81.8 13.8 %collective-permute-done.3 = f32[32,256]{1,0:T(8,128)S(1)} collective-permute-done((f32[32,256]{1,0:T(8,128)S(1)}, f32[32,256]{1,0:T(8,128)S(1)}, u32[]{:S(2)}, u32[]{:S(2)}) %collective-permute-start.3) | collective-permute-done | bytes 32800 | tf_op jit(solution)/shard_map/ppermute | solution.py:211
  95.6 0.0 collective-permute-start.4
  95.6 5.2 %collective-permute-done.4 = f32[32,256]{1,0:T(8,128)S(1)} collective-permute-done((f32[32,256]{1,0:T(8,128)S(1)}, f32[32,256]{1,0:T(8,128)S(1)}, u32[]{:S(2)}, u32[]{:S(2)}) %collective-permute-start.4) | collective-permute-done | bytes 32800 | tf_op jit(solution)/shard_map/ppermute | solution.py:211
  100.8 0.3 collective-permute-start.5
  101.1 3.6 %collective-permute-done.5 = f32[32,256]{1,0:T(8,128)S(1)} collective-permute-done((f32[32,256]{1,0:T(8,128)S(1)}, f32[32,256]{1,0:T(8,128)S(1)}, u32[]{:S(2)}, u32[]{:S(2)}) %collective-permute-start.5) | collective-permute-done | bytes 32800 | tf_op jit(solution)/shard_map/ppermute | solution.py:211
  104.7 0.0 collective-permute-start.6
  104.7 3.9 %collective-permute-done.6 = f32[32,256]{1,0:T(8,128)S(1)} collective-permute-done((f32[32,256]{1,0:T(8,128)S(1)}, f32[32,256]{1,0:T(8,128)S(1)}, u32[]{:S(2)}, u32[]{:S(2)}) %collective-permute-start.6) | collective-permute-done | bytes 32800 | tf_op jit(solution)/shard_map/ppermute | solution.py:211
  108.6 2.1 %collective-permute-start.7 = (f32[32,256]{1,0:T(8,128)S(1)}, f32[32,256]{1,0:T(8,128)S(1)}, u32[]{:S(2)}, u32[]{:S(2)}) collective-permute-start(f32[32,256]{1,0:T(8,128)S(1)} %add.20), channel_id=1, source_target_pairs={{0,16},{8,24},{16,0},{24,8},{1,17},{9,25},{17,1},{25,9},{2,18},{10... | collective-permute-start | bytes 98312 | tf_op jit(solution)/shard_map/ppermute | solution.py:211
  110.7 3.3 %collective-permute-done.7 = f32[32,256]{1,0:T(8,128)S(1)} collective-permute-done((f32[32,256]{1,0:T(8,128)S(1)}, f32[32,256]{1,0:T(8,128)S(1)}, u32[]{:S(2)}, u32[]{:S(2)}) %collective-permute-start.7) | collective-permute-done | bytes 32800 | tf_op jit(solution)/shard_map/ppermute | solution.py:211
  114.1 0.2 fit.1
  114.2 0.0 all-to-all-done.3
  114.2 0.1 convert_element_type.40
  114.3 0.3 fusion.6
  114.7 0.1 fusion
  114.8 0.6 bitcast_bitcast_fusion
  (13 shorter events, 0.1 us)
Async XLA Ops:
  0.0 0.7 copy-start
  0.0 13.3 %copy-start.1 = (s32[2,3]{1,0:T(2,128)S(1)}, s32[2,3]{1,0:T(2,128)}, u32[]{:S(2)}) copy-start(s32[2,3]{1,0:T(2,128)} %triples.1) | copy-start | bytes 76
  1.6 28.5 %all-to-all-start = ((bf16[32,2,32,128]{3,2,1,0:T(8,128)(2,1)}), bf16[32,2,32,128]{3,2,1,0:T(8,128)(2,1)S(1)}, u32[]{:S(2)}, u32[]{:S(2)}) async-start(bf16[32,2,32,128]{3,2,1,0:T(8,128)(2,1)} %broadcast_in_dim.10), calls=%async_computation | async-start | bytes 1048576 | tf_op jit(solution)/shard_map/all_to_all | solution.py:238
  13.5 1.2 %collective-permute-start = (bf16[1,80,128]{2,1,0:T(8,128)(2,1)S(1)}, bf16[1,80,128]{2,1,0:T(8,128)(2,1)S(1)}, u32[]{:S(2)}, u32[]{:S(2)}) collective-permute-start(bf16[1,80,128]{2,1,0:T(8,128)(2,1)S(1)} %fusion.3), channel_id=1, source_target_pairs={{0,1},{1,0},{2,3},{3,2},{4,5},{5,4},{6,7},{7,6},{8,9},{9,8},{10,11... | collective-permute-start | bytes 61448 | tf_op jit(solution)/shard_map/ppermute | solution.py:211
  14.7 4.0 %collective-permute-start.1 = (bf16[2,80,128]{2,1,0:T(8,128)(2,1)S(1)}, bf16[2,80,128]{2,1,0:T(8,128)(2,1)S(1)}, u32[]{:S(2)}, u32[]{:S(2)}) collective-permute-start(bf16[2,80,128]{2,1,0:T(8,128)(2,1)S(1)} %pad_maximum_fusion.2), channel_id=1, source_target_pairs={{0,2},{1,3},{2,0},{3,1},{4,6},{5,7},{6,4},{7,5},{8,10},{9,11},{10,... | collective-permute-start | bytes 122888 | tf_op jit(solution)/shard_map/ppermute | solution.py:211
  18.7 6.0 %collective-permute-start.2 = (bf16[4,80,128]{2,1,0:T(8,128)(2,1)S(1)}, bf16[4,80,128]{2,1,0:T(8,128)(2,1)S(1)}, u32[]{:S(2)}, u32[]{:S(2)}) collective-permute-start(bf16[4,80,128]{2,1,0:T(8,128)(2,1)S(1)} %pad_maximum_fusion.1), channel_id=1, source_target_pairs={{0,4},{1,5},{2,6},{3,7},{4,0},{5,1},{6,2},{7,3},{8,12},{9,13},{10,... | collective-permute-start | bytes 245768 | tf_op jit(solution)/shard_map/ppermute | solution.py:211
  31.6 13.2 %all-to-all-start.1 = ((bf16[8,6,32,128]{3,2,1,0:T(8,128)(2,1)}), bf16[8,6,32,128]{3,2,1,0:T(8,128)(2,1)S(1)}, u32[]{:S(2)}, u32[]{:S(2)}) async-start(bf16[8,6,32,128]{3,2,1,0:T(8,128)(2,1)} %select.8), calls=%async_computation.1 | async-start | bytes 786432 | tf_op jit(solution)/shard_map/all_to_all | solution.py:263
  70.6 43.6 %all-to-all-start.3 = ((f16[32,72,128]{2,1,0:T(8,128)(2,1)}), f16[32,72,128]{2,1,0:T(8,128)(2,1)S(1)}, u32[]{:S(2)}, u32[]{:S(2)}) async-start(f16[32,72,128]{2,1,0:T(8,128)(2,1)} %convert_element_type.39), calls=%async_computation.3 | async-start | bytes 1179648 | tf_op jit(solution)/shard_map/all_to_all | solution.py:315
  76.4 19.2 %collective-permute-start.3 = (f32[32,256]{1,0:T(8,128)S(1)}, f32[32,256]{1,0:T(8,128)S(1)}, u32[]{:S(2)}, u32[]{:S(2)}) collective-permute-start(f32[32,256]{1,0:T(8,128)S(1)} %gram.1), channel_id=1, source_target_pairs={{0,128},{32,160},{64,192},{96,224},{128,0},{160,32},{192,64},{224,... | collective-permute-start | bytes 98312 | tf_op jit(solution)/shard_map/ppermute | solution.py:211
  95.6 5.2 %collective-permute-start.4 = (f32[32,256]{1,0:T(8,128)S(1)}, f32[32,256]{1,0:T(8,128)S(1)}, u32[]{:S(2)}, u32[]{:S(2)}) collective-permute-start(f32[32,256]{1,0:T(8,128)S(1)} %add.17), channel_id=1, source_target_pairs={{0,64},{32,96},{64,0},{96,32},{128,192},{160,224},{192,128},{224,1... | collective-permute-start | bytes 98312 | tf_op jit(solution)/shard_map/ppermute | solution.py:211
  100.8 3.9 %collective-permute-start.5 = (f32[32,256]{1,0:T(8,128)S(1)}, f32[32,256]{1,0:T(8,128)S(1)}, u32[]{:S(2)}, u32[]{:S(2)}) collective-permute-start(f32[32,256]{1,0:T(8,128)S(1)} %add.18), channel_id=1, source_target_pairs={{0,32},{32,0},{64,96},{96,64},{128,160},{160,128},{192,224},{224,1... | collective-permute-start | bytes 98312 | tf_op jit(solution)/shard_map/ppermute | solution.py:211
  104.7 3.9 %collective-permute-start.6 = (f32[32,256]{1,0:T(8,128)S(1)}, f32[32,256]{1,0:T(8,128)S(1)}, u32[]{:S(2)}, u32[]{:S(2)}) collective-permute-start(f32[32,256]{1,0:T(8,128)S(1)} %add.19), channel_id=1, source_target_pairs={{0,8},{8,0},{16,24},{24,16},{1,9},{9,1},{17,25},{25,17},{2,10},{10... | collective-permute-start | bytes 98312 | tf_op jit(solution)/shard_map/ppermute | solution.py:211
  108.6 5.4 %collective-permute-start.7 = (f32[32,256]{1,0:T(8,128)S(1)}, f32[32,256]{1,0:T(8,128)S(1)}, u32[]{:S(2)}, u32[]{:S(2)}) collective-permute-start(f32[32,256]{1,0:T(8,128)S(1)} %add.20), channel_id=1, source_target_pairs={{0,16},{8,24},{16,0},{24,8},{1,17},{9,25},{17,1},{25,9},{2,18},{10... | collective-permute-start | bytes 98312 | tf_op jit(solution)/shard_map/ppermute | solution.py:211

commit v5 on v4

--- a/solution.py
+++ b/solution.py
@@ -77,7 +77,7 @@
 
 
 def contract_kernel(
-    triples, count, x_far, sel, out,
+    triples, count, head, x_far, sel, out,
     x, arrived, fac, low, mid, y1, y2, y3,
 ):
     slots = x.shape[0]
@@ -86,7 +86,8 @@
     per_slot = BS // CHUNK
     chunks = slots * per_slot
     pieces = chunks // PIECE
-    for piece in range(min(AHEAD, pieces)):
+    skipped = STEP // PIECE
+    for piece in range(skipped, skipped + AHEAD):
         fetch(x_far, x, arrived, piece).start()
     for slot in range(slots):
         for side in range(3):
@@ -100,24 +101,18 @@
     y2[...] = jnp.zeros_like(y2)
     y3[...] = jnp.zeros_like(y3)
 
-    def several(step, carry):
-        for n in range(STEP // PIECE):
-            piece = step * (STEP // PIECE) + n
-
-            @pl.when(piece + AHEAD < pieces)
-            def _():
-                fetch(x_far, x, arrived, piece + AHEAD).start()
-
-            fetch(x_far, x, arrived, piece).wait()
+    def several(step, source):
         for n in range(STEP):
             chunk = step * STEP + n
             slot = chunk // per_slot
-            row0 = pl.multiple_of(lax.rem(chunk, per_slot) * CHUNK, CHUNK)
+            row0 = (chunk - slot * per_slot) * CHUNK
+            if not isinstance(row0, int):
+                row0 = pl.multiple_of(row0, CHUNK)
             lower = low[slot]
             middle = mid[slot]
             firsts = [[] for _ in range(rank // BS)]
             for a0 in range(0, CHUNK, GROUP):
-                blocks = x[slot, pl.ds(row0 + a0, GROUP)]
+                blocks = source(slot, pl.ds(row0 + a0, GROUP))
                 ls = jnp.dot(
                     blocks.reshape(GROUP * BS, BS), lower, preferred_element_type=F32
                 ).reshape(GROUP, BS, rank)
@@ -147,9 +142,22 @@
             for half in range(rank // BS):
                 cols = slice(half * BS, (half + 1) * BS)
                 y1[slot, pl.ds(row0, CHUNK), cols] = jnp.concatenate(firsts[half], axis=0)
+
+    several(0, lambda slot, rows: head[rows])
+
+    def later(step, carry):
+        for n in range(STEP // PIECE):
+            piece = step * (STEP // PIECE) + n
+
+            @pl.when(piece + AHEAD < pieces)
+            def _():
+                fetch(x_far, x, arrived, piece + AHEAD).start()
+
+            fetch(x_far, x, arrived, piece).wait()
+        several(step, lambda slot, rows: x[slot, rows])
         return carry
 
-    lax.fori_loop(0, chunks // STEP, several, 0)
+    lax.fori_loop(1, chunks // STEP, later, 0)
 
     scaled = []
     top = jnp.zeros((1, 1), F32)
@@ -266,10 +274,11 @@
     gram = summed(gram, "blk_0", (2,))
     gram = summed(gram, "blk_0", (1,))
 
+    head = tensor_blocks[0, : STEP * CHUNK]
     parts = pl.pallas_call(
         contract_kernel,
         out_shape=VMEM((reps, named * width + SUBLANES, BS), F32),
-        in_specs=[whole(SMEM), whole(SMEM), whole(pltpu.HBM), whole()],
+        in_specs=[whole(SMEM), whole(SMEM), whole(), whole(pltpu.HBM), whole()],
         out_specs=whole(),
         scratch_shapes=[
             VMEM((slots, BS, BS, BS), BF16),
@@ -286,6 +295,7 @@
     )(
         triples,
         slot_count,
+        near(head),
         pltpu.with_memory_space_constraint(tensor_blocks, pltpu.HBM),
         near(chosen),
     )

time: 116 us -> 116 us (level)
  waiting for transfers between devices: 50.1 us -> 47.7 us
  local copies, waits for them, and re-layouts: 1.73 us -> 3.47 us
    all_to_all x1, waiting for transfers between devices: 8.26 us -> 6.51 us  [shards(): chosen = lax.all_to_all(chosen, 'rep', 0, 0, tiled=True)]
    squeeze x0 -> x1, local copies, waits for them, and re-layouts: none -> 1.73 us  [shards(): head = tensor_blocks[0, :STEP * CHUNK]]
  transfers between devices with their start and end apart: 11 -> 11, of which waited for: 10 -> 10; matrix products, arithmetic and copies ran while one was open for 0% -> 2% of each run, Pallas kernels for 0% -> 0%
where the time goes in v5:
time: 116 us
  waiting for transfers between devices  47.7 us (41%)
  starting transfers between devices  34.1 us (29%)
  Pallas kernels  15.2 us (13%)
  blocking collectives  11.5 us (10%)
  local copies, waits for them, and re-layouts  3.47 us (3%)
  other arithmetic  2.93 us (3%)
    ppermute x8, waiting for transfers between devices, swapped(): return lax.ppermute(array, axis, [(i, i ^ bit) for i in range(peers)])  36.4 us
    ppermute x8, starting transfers between devices, swapped(): return lax.ppermute(array, axis, [(i, i ^ bit) for i in range(peers)])  12.5 us
    pallas_call x1, Pallas kernels, shards(): pl.pallas_call(contract_kernel, out_shape=VMEM((reps, named * width + SUB...  12.4 us
    all_to_all x1, starting transfers between devices, shards(): lax.all_to_all(jnp.broadcast_to(own[None], (owners, *own.shape)), BLK, 0,...  11.7 us
    all_to_all x1, blocking collectives, shards(): parts = lax.all_to_all(parts.astype(F16), 'rep', 0, 0, tiled=True)  11.5 us
    all_to_all x1, waiting for transfers between devices, shards(): chosen = lax.all_to_all(chosen, 'rep', 0, 0, tiled=True)  6.51 us
    all_to_all x1, starting transfers between devices, shards(): arrived = lax.all_to_all(scaled.astype(F16), BLK, 0, 0, tiled=True)  5.57 us
    all_to_all x1, waiting for transfers between devices, shards(): lax.all_to_all(jnp.broadcast_to(own[None], (owners, *own.shape)), BLK, 0,...  4.74 us
  transfers between devices with their start and end apart: 11, of which 10 were waited for; matrix products, arithmetic and copies ran while one was open for 2% of the time, Pallas kernels for 0%

profile of v5, /device:TPU:8, one launch (start us, length us, event | category | flops | bytes accessed | tf_op | source)
XLA Modules:
  0.0 115.6 jit_solution(3946620255017432345)
XLA Ops:
  0.0 0.0 copy-start
  0.0 0.7 copy-done
  0.7 0.9 broadcast_in_dim.10
  1.6 11.7 %all-to-all-start = ((bf16[32,2,32,128]{3,2,1,0:T(8,128)(2,1)}), bf16[32,2,32,128]{3,2,1,0:T(8,128)(2,1)S(1)}, u32[]{:S(2)}, u32[]{:S(2)}) async-start(bf16[32,2,32,128]{3,2,1,0:T(8,128)(2,1)} %broadcast_in_dim.10), calls=%async_computation | async-start | bytes 1048576 | tf_op jit(solution)/shard_map/all_to_all | solution.py:246
  13.3 0.7 convert_element_type.33
  14.0 0.1 convert_element_type.34
  14.1 0.1 collective-permute-start
  14.2 1.2 %collective-permute-done = bf16[1,80,128]{2,1,0:T(8,128)(2,1)S(1)} collective-permute-done((bf16[1,80,128]{2,1,0:T(8,128)(2,1)S(1)}, bf16[1,80,128]{2,1,0:T(8,128)(2,1)S(1)}, u32[]{:S(2)}, u32[]{:S(2)}) %collective-permute-start) | collective-permute-done | bytes 20512 | tf_op jit(solution)/shard_map/ppermute | solution.py:219
  15.4 1.5 %collective-permute-start.1 = (bf16[2,80,128]{2,1,0:T(8,128)(2,1)S(1)}, bf16[2,80,128]{2,1,0:T(8,128)(2,1)S(1)}, u32[]{:S(2)}, u32[]{:S(2)}) collective-permute-start(bf16[2,80,128]{2,1,0:T(8,128)(2,1)S(1)} %pad_maximum_fusion.2), channel_id=1, source_target_pairs={{0,2},{1,3},{2,0},{3,1},{4,6},{5,7},{6,4},{7,5},{8,10},{9,11},{10,... | collective-permute-start | bytes 122888 | tf_op jit(solution)/shard_map/ppermute | solution.py:219
  16.9 2.5 %collective-permute-done.1 = bf16[2,80,128]{2,1,0:T(8,128)(2,1)S(1)} collective-permute-done((bf16[2,80,128]{2,1,0:T(8,128)(2,1)S(1)}, bf16[2,80,128]{2,1,0:T(8,128)(2,1)S(1)}, u32[]{:S(2)}, u32[]{:S(2)}) %collective-permute-start.1) | collective-permute-done | bytes 40992 | tf_op jit(solution)/shard_map/ppermute | solution.py:219
  19.4 3.1 %collective-permute-start.2 = (bf16[4,80,128]{2,1,0:T(8,128)(2,1)S(1)}, bf16[4,80,128]{2,1,0:T(8,128)(2,1)S(1)}, u32[]{:S(2)}, u32[]{:S(2)}) collective-permute-start(bf16[4,80,128]{2,1,0:T(8,128)(2,1)S(1)} %pad_maximum_fusion.1), channel_id=1, source_target_pairs={{0,4},{1,5},{2,6},{3,7},{4,0},{5,1},{6,2},{7,3},{8,12},{9,13},{10,... | collective-permute-start | bytes 245768 | tf_op jit(solution)/shard_map/ppermute | solution.py:219
  22.5 2.9 %collective-permute-done.2 = bf16[4,80,128]{2,1,0:T(8,128)(2,1)S(1)} collective-permute-done((bf16[4,80,128]{2,1,0:T(8,128)(2,1)S(1)}, bf16[4,80,128]{2,1,0:T(8,128)(2,1)S(1)}, u32[]{:S(2)}, u32[]{:S(2)}) %collective-permute-start.2) | collective-permute-done | bytes 81952 | tf_op jit(solution)/shard_map/ppermute | solution.py:219
  25.4 4.7 %all-to-all-done = bf16[32,2,32,128]{3,2,1,0:T(8,128)(2,1)S(1)} async-done(((bf16[32,2,32,128]{3,2,1,0:T(8,128)(2,1)}), bf16[32,2,32,128]{3,2,1,0:T(8,128)(2,1)S(1)}, u32[]{:S(2)}, u32[]{:S(2)}) %all-to-all-start) | async-done | bytes 524320 | tf_op jit(solution)/shard_map/all_to_all | solution.py:246
  30.2 1.4 %select.8 = bf16[8,6,32,128]{3,2,1,0:T(8,128)(2,1)} custom-call(s32[8,6]{1,0:T(8,128)S(1)} %bitcast.32, s32[1]{0:T(128)} %bitcast.6.place, bf16[64,32,128]{2,1,0:T(8,128)(2,1)S(1)} %bitcast.29), custom_call_target="tpu_custom_call" | custom-call | tf_op jit(solution)/shard_map/select/pallas_call | solution.py:263
  31.6 4.3 %all-to-all-start.1 = ((bf16[8,6,32,128]{3,2,1,0:T(8,128)(2,1)}), bf16[8,6,32,128]{3,2,1,0:T(8,128)(2,1)S(1)}, u32[]{:S(2)}, u32[]{:S(2)}) async-start(bf16[8,6,32,128]{3,2,1,0:T(8,128)(2,1)} %select.8), calls=%async_computation.1 | async-start | bytes 786432 | tf_op jit(solution)/shard_map/all_to_all | solution.py:271
  36.5 0.0 copy-start.1
  36.5 1.7 %slice_bitcast_fusion.head = bf16[64,128,128]{2,1,0:T(8,128)(2,1)S(1)} fusion(bf16[2,128,128,128]{3,2,1,0:T(8,128)(2,1)} %x_far.1), kind=kLoop, calls=%fused_computation | loop fusion | bytes 4194304 | tf_op jit(solution)/shard_map/squeeze | solution.py:277
  38.3 6.5 %all-to-all-done.1.sel = bf16[8,6,32,128]{3,2,1,0:T(8,128)(2,1)S(1)} async-done(((bf16[8,6,32,128]{3,2,1,0:T(8,128)(2,1)}), bf16[8,6,32,128]{3,2,1,0:T(8,128)(2,1)S(1)}, u32[]{:S(2)}, u32[]{:S(2)}) %all-to-all-start.1) | async-done | bytes 393248 | tf_op jit(solution)/shard_map/all_to_all | solution.py:271
  44.8 0.0 copy-done.1
  44.8 12.4 %contract.1 = f32[8,200,128]{2,1,0:T(8,128)S(1)} custom-call(s32[2,3]{1,0:T(2,128)S(1)} %copy-done.1, s32[1]{0:T(128)S(6)} %copy.15.count, bf16[64,128,128]{2,1,0:T(8,128)(2,1)S(1)} %slice_bitcast_fusion.head, bf16[2,128,128,128]{3,2,1,0:T(8,128)(2,1)} %x_far.1, bf16[8,6,32,128]{3,2,1,0:T(8,128)(2,1)S(1)} %all-to-all-done.1.sel), custom_call_target="tpu_custom_call" | custom-call | tf_op jit(solution)/shard_map/contract/pallas_call | solution.py:278
  57.2 0.1 convert_element_type.37
  57.3 11.5 %all_to_all.20 = f16[8,200,128]{2,1,0:T(8,128)(2,1)S(1)} all-to-all(f16[8,200,128]{2,1,0:T(8,128)(2,1)S(1)} %convert_element_type.37), channel_id=1, replica_groups=mesh['blk_0'=8,'blk_1'=4,'rep'=8] {'rep'}, dimensions={0} | all-to-all | bytes 819200 | tf_op jit(solution)/shard_map/all_to_all | solution.py:302
  68.8 0.1 convert_element_type.38.parts
  68.8 1.1 scatter.1
  69.9 0.9 convert_element_type.39
  70.8 5.6 %all-to-all-start.3 = ((f16[32,72,128]{2,1,0:T(8,128)(2,1)}), f16[32,72,128]{2,1,0:T(8,128)(2,1)S(1)}, u32[]{:S(2)}, u32[]{:S(2)}) async-start(f16[32,72,128]{2,1,0:T(8,128)(2,1)} %convert_element_type.39), calls=%async_computation.3 | async-start | bytes 1179648 | tf_op jit(solution)/shard_map/all_to_all | solution.py:325
  76.4 0.1 gram.1
  76.6 5.4 %collective-permute-start.3 = (f32[32,256]{1,0:T(8,128)S(1)}, f32[32,256]{1,0:T(8,128)S(1)}, u32[]{:S(2)}, u32[]{:S(2)}) collective-permute-start(f32[32,256]{1,0:T(8,128)S(1)} %gram.1), channel_id=1, source_target_pairs={{0,128},{32,160},{64,192},{96,224},{128,0},{160,32},{192,64},{224,... | collective-permute-start | bytes 98312 | tf_op jit(solution)/shard_map/ppermute | solution.py:219
  82.0 13.8 %collective-permute-done.3 = f32[32,256]{1,0:T(8,128)S(1)} collective-permute-done((f32[32,256]{1,0:T(8,128)S(1)}, f32[32,256]{1,0:T(8,128)S(1)}, u32[]{:S(2)}, u32[]{:S(2)}) %collective-permute-start.3) | collective-permute-done | bytes 32800 | tf_op jit(solution)/shard_map/ppermute | solution.py:219
  95.8 0.0 collective-permute-start.4
  95.8 5.2 %collective-permute-done.4 = f32[32,256]{1,0:T(8,128)S(1)} collective-permute-done((f32[32,256]{1,0:T(8,128)S(1)}, f32[32,256]{1,0:T(8,128)S(1)}, u32[]{:S(2)}, u32[]{:S(2)}) %collective-permute-start.4) | collective-permute-done | bytes 32800 | tf_op jit(solution)/shard_map/ppermute | solution.py:219
  101.0 0.3 collective-permute-start.5
  101.3 3.6 %collective-permute-done.5 = f32[32,256]{1,0:T(8,128)S(1)} collective-permute-done((f32[32,256]{1,0:T(8,128)S(1)}, f32[32,256]{1,0:T(8,128)S(1)}, u32[]{:S(2)}, u32[]{:S(2)}) %collective-permute-start.5) | collective-permute-done | bytes 32800 | tf_op jit(solution)/shard_map/ppermute | solution.py:219
  104.9 0.0 collective-permute-start.6
  104.9 3.9 %collective-permute-done.6 = f32[32,256]{1,0:T(8,128)S(1)} collective-permute-done((f32[32,256]{1,0:T(8,128)S(1)}, f32[32,256]{1,0:T(8,128)S(1)}, u32[]{:S(2)}, u32[]{:S(2)}) %collective-permute-start.6) | collective-permute-done | bytes 32800 | tf_op jit(solution)/shard_map/ppermute | solution.py:219
  108.8 2.1 %collective-permute-start.7 = (f32[32,256]{1,0:T(8,128)S(1)}, f32[32,256]{1,0:T(8,128)S(1)}, u32[]{:S(2)}, u32[]{:S(2)}) collective-permute-start(f32[32,256]{1,0:T(8,128)S(1)} %add.20), channel_id=1, source_target_pairs={{0,16},{8,24},{16,0},{24,8},{1,17},{9,25},{17,1},{25,9},{2,18},{10... | collective-permute-start | bytes 98312 | tf_op jit(solution)/shard_map/ppermute | solution.py:219
  110.9 3.3 %collective-permute-done.7 = f32[32,256]{1,0:T(8,128)S(1)} collective-permute-done((f32[32,256]{1,0:T(8,128)S(1)}, f32[32,256]{1,0:T(8,128)S(1)}, u32[]{:S(2)}, u32[]{:S(2)}) %collective-permute-start.7) | collective-permute-done | bytes 32800 | tf_op jit(solution)/shard_map/ppermute | solution.py:219
  114.3 0.2 fit.1
  114.4 0.0 all-to-all-done.3
  114.4 0.1 convert_element_type.40
  114.5 0.3 fusion.6
  114.9 0.1 fusion
  115.0 0.6 bitcast_bitcast_fusion
  (12 shorter events, 0.1 us)
Async XLA Ops:
  0.0 0.7 copy-start
  1.6 28.5 %all-to-all-start = ((bf16[32,2,32,128]{3,2,1,0:T(8,128)(2,1)}), bf16[32,2,32,128]{3,2,1,0:T(8,128)(2,1)S(1)}, u32[]{:S(2)}, u32[]{:S(2)}) async-start(bf16[32,2,32,128]{3,2,1,0:T(8,128)(2,1)} %broadcast_in_dim.10), calls=%async_computation | async-start | bytes 1048576 | tf_op jit(solution)/shard_map/all_to_all | solution.py:246
  14.1 1.2 %collective-permute-start = (bf16[1,80,128]{2,1,0:T(8,128)(2,1)S(1)}, bf16[1,80,128]{2,1,0:T(8,128)(2,1)S(1)}, u32[]{:S(2)}, u32[]{:S(2)}) collective-permute-start(bf16[1,80,128]{2,1,0:T(8,128)(2,1)S(1)} %fusion.3), channel_id=1, source_target_pairs={{0,1},{1,0},{2,3},{3,2},{4,5},{5,4},{6,7},{7,6},{8,9},{9,8},{10,11... | collective-permute-start | bytes 61448 | tf_op jit(solution)/shard_map/ppermute | solution.py:219
  15.4 4.0 %collective-permute-start.1 = (bf16[2,80,128]{2,1,0:T(8,128)(2,1)S(1)}, bf16[2,80,128]{2,1,0:T(8,128)(2,1)S(1)}, u32[]{:S(2)}, u32[]{:S(2)}) collective-permute-start(bf16[2,80,128]{2,1,0:T(8,128)(2,1)S(1)} %pad_maximum_fusion.2), channel_id=1, source_target_pairs={{0,2},{1,3},{2,0},{3,1},{4,6},{5,7},{6,4},{7,5},{8,10},{9,11},{10,... | collective-permute-start | bytes 122888 | tf_op jit(solution)/shard_map/ppermute | solution.py:219
  19.4 6.0 %collective-permute-start.2 = (bf16[4,80,128]{2,1,0:T(8,128)(2,1)S(1)}, bf16[4,80,128]{2,1,0:T(8,128)(2,1)S(1)}, u32[]{:S(2)}, u32[]{:S(2)}) collective-permute-start(bf16[4,80,128]{2,1,0:T(8,128)(2,1)S(1)} %pad_maximum_fusion.1), channel_id=1, source_target_pairs={{0,4},{1,5},{2,6},{3,7},{4,0},{5,1},{6,2},{7,3},{8,12},{9,13},{10,... | collective-permute-start | bytes 245768 | tf_op jit(solution)/shard_map/ppermute | solution.py:219
  31.6 13.2 %all-to-all-start.1 = ((bf16[8,6,32,128]{3,2,1,0:T(8,128)(2,1)}), bf16[8,6,32,128]{3,2,1,0:T(8,128)(2,1)S(1)}, u32[]{:S(2)}, u32[]{:S(2)}) async-start(bf16[8,6,32,128]{3,2,1,0:T(8,128)(2,1)} %select.8), calls=%async_computation.1 | async-start | bytes 786432 | tf_op jit(solution)/shard_map/all_to_all | solution.py:271
  36.5 8.3 %copy-start.1 = (s32[2,3]{1,0:T(2,128)S(1)}, s32[2,3]{1,0:T(2,128)}, u32[]{:S(2)}) copy-start(s32[2,3]{1,0:T(2,128)} %triples.1) | copy-start | bytes 76
  70.8 43.6 %all-to-all-start.3 = ((f16[32,72,128]{2,1,0:T(8,128)(2,1)}), f16[32,72,128]{2,1,0:T(8,128)(2,1)S(1)}, u32[]{:S(2)}, u32[]{:S(2)}) async-start(f16[32,72,128]{2,1,0:T(8,128)(2,1)} %convert_element_type.39), calls=%async_computation.3 | async-start | bytes 1179648 | tf_op jit(solution)/shard_map/all_to_all | solution.py:325
  76.6 19.2 %collective-permute-start.3 = (f32[32,256]{1,0:T(8,128)S(1)}, f32[32,256]{1,0:T(8,128)S(1)}, u32[]{:S(2)}, u32[]{:S(2)}) collective-permute-start(f32[32,256]{1,0:T(8,128)S(1)} %gram.1), channel_id=1, source_target_pairs={{0,128},{32,160},{64,192},{96,224},{128,0},{160,32},{192,64},{224,... | collective-permute-start | bytes 98312 | tf_op jit(solution)/shard_map/ppermute | solution.py:219
  95.8 5.2 %collective-permute-start.4 = (f32[32,256]{1,0:T(8,128)S(1)}, f32[32,256]{1,0:T(8,128)S(1)}, u32[]{:S(2)}, u32[]{:S(2)}) collective-permute-start(f32[32,256]{1,0:T(8,128)S(1)} %add.17), channel_id=1, source_target_pairs={{0,64},{32,96},{64,0},{96,32},{128,192},{160,224},{192,128},{224,1... | collective-permute-start | bytes 98312 | tf_op jit(solution)/shard_map/ppermute | solution.py:219
  101.0 3.9 %collective-permute-start.5 = (f32[32,256]{1,0:T(8,128)S(1)}, f32[32,256]{1,0:T(8,128)S(1)}, u32[]{:S(2)}, u32[]{:S(2)}) collective-permute-start(f32[32,256]{1,0:T(8,128)S(1)} %add.18), channel_id=1, source_target_pairs={{0,32},{32,0},{64,96},{96,64},{128,160},{160,128},{192,224},{224,1... | collective-permute-start | bytes 98312 | tf_op jit(solution)/shard_map/ppermute | solution.py:219
  104.9 3.9 %collective-permute-start.6 = (f32[32,256]{1,0:T(8,128)S(1)}, f32[32,256]{1,0:T(8,128)S(1)}, u32[]{:S(2)}, u32[]{:S(2)}) collective-permute-start(f32[32,256]{1,0:T(8,128)S(1)} %add.19), channel_id=1, source_target_pairs={{0,8},{8,0},{16,24},{24,16},{1,9},{9,1},{17,25},{25,17},{2,10},{10... | collective-permute-start | bytes 98312 | tf_op jit(solution)/shard_map/ppermute | solution.py:219
  108.8 5.4 %collective-permute-start.7 = (f32[32,256]{1,0:T(8,128)S(1)}, f32[32,256]{1,0:T(8,128)S(1)}, u32[]{:S(2)}, u32[]{:S(2)}) collective-permute-start(f32[32,256]{1,0:T(8,128)S(1)} %add.20), channel_id=1, source_target_pairs={{0,16},{8,24},{16,0},{24,8},{1,17},{9,25},{17,1},{25,9},{2,18},{10... | collective-permute-start | bytes 98312 | tf_op jit(solution)/shard_map/ppermute | solution.py:219

commit v6 on v4

--- a/solution.py
+++ b/solution.py
@@ -77,7 +77,7 @@
 
 
 def contract_kernel(
-    triples, count, x_far, sel, out,
+    triples, count, head, x_far, sel, out,
     x, arrived, fac, low, mid, y1, y2, y3,
 ):
     slots = x.shape[0]
@@ -86,8 +86,16 @@
     per_slot = BS // CHUNK
     chunks = slots * per_slot
     pieces = chunks // PIECE
-    for piece in range(min(AHEAD, pieces)):
+    skipped = STEP // PIECE
+    for piece in range(skipped, skipped + AHEAD):
         fetch(x_far, x, arrived, piece).start()
+
+    def placed(n, carry):
+        rows = pl.ds(pl.multiple_of(n * CHUNK, CHUNK), CHUNK)
+        x[0, rows] = head[rows]
+        return carry
+
+    lax.fori_loop(0, STEP, placed, 0)
     for slot in range(slots):
         for side in range(3):
             turned = sel[:, slot * 3 + side].reshape(rank, BS).astype(F32).T
@@ -104,11 +112,14 @@
         for n in range(STEP // PIECE):
             piece = step * (STEP // PIECE) + n
 
-            @pl.when(piece + AHEAD < pieces)
+            @pl.when((step > 0) & (piece + AHEAD < pieces))
             def _():
                 fetch(x_far, x, arrived, piece + AHEAD).start()
 
-            fetch(x_far, x, arrived, piece).wait()
+            @pl.when(step > 0)
+            def _():
+                fetch(x_far, x, arrived, piece).wait()
+
         for n in range(STEP):
             chunk = step * STEP + n
             slot = chunk // per_slot
@@ -262,14 +273,15 @@
     )(names, place, near(table))
     chosen = lax.all_to_all(chosen, "rep", 0, 0, tiled=True)
 
-    gram = summed(gram, "blk_0", (4,))
+    gram = summed(gram, "blk_1", (1,))
     gram = summed(gram, "blk_0", (2,))
     gram = summed(gram, "blk_0", (1,))
 
+    head = tensor_blocks[0, : STEP * CHUNK]
     parts = pl.pallas_call(
         contract_kernel,
         out_shape=VMEM((reps, named * width + SUBLANES, BS), F32),
-        in_specs=[whole(SMEM), whole(SMEM), whole(pltpu.HBM), whole()],
+        in_specs=[whole(SMEM), whole(SMEM), whole(), whole(pltpu.HBM), whole()],
         out_specs=whole(),
         scratch_shapes=[
             VMEM((slots, BS, BS, BS), BF16),
@@ -286,12 +298,13 @@
     )(
         triples,
         slot_count,
+        near(head),
         pltpu.with_memory_space_constraint(tensor_blocks, pltpu.HBM),
         near(chosen),
     )
     parts = lax.all_to_all(parts.astype(F16), "rep", 0, 0, tiled=True)
 
-    gram = summed(gram, "blk_1", (1,))
+    gram = summed(gram, "blk_0", (4,))
     gram = summed(gram, "blk_1", (2,))
     fitted = pl.pallas_call(
         fit_kernel,

time: 116 us -> 110 us (0.948)
  waiting for transfers between devices: 50.1 us -> 41.5 us
  local copies, waits for them, and re-layouts: 1.73 us -> 3.47 us
  starting transfers between devices: 34.1 us -> 35.4 us
  Pallas kernels: 15 us -> 13.8 us
    ppermute x8, waiting for transfers between devices: 36.4 us -> 30.2 us  [swapped(): return lax.ppermute(array, axis, [(i, i ^ bit) for i in range(peers)])]
    all_to_all x1, waiting for transfers between devices: 8.26 us -> 6.51 us  [shards(): chosen = lax.all_to_all(chosen, 'rep', 0, 0, tiled=True)]
    squeeze x0 -> x1, local copies, waits for them, and re-layouts: none -> 1.73 us  [shards(): head = tensor_blocks[0, :STEP * CHUNK]]
    ppermute x8, starting transfers between devices: 12.5 us -> 13.8 us  [swapped(): return lax.ppermute(array, axis, [(i, i ^ bit) for i in range(peers)])]
    pallas_call x1, Pallas kernels: 12.2 us -> 11 us  [shards(): pl.pallas_call(contract_kernel, out_shape=VMEM((reps, named * width + SUB...]
  transfers between devices with their start and end apart: 11 -> 11, of which waited for: 10 -> 10; matrix products, arithmetic and copies ran while one was open for 0% -> 2% of each run, Pallas kernels for 0% -> 0%
where the time goes in v6:
time: 110 us; the launch traced here: 109 us
  waiting for transfers between devices  41.5 us (38%)
  starting transfers between devices  35.4 us (32%)
  Pallas kernels  13.8 us (13%)
  blocking collectives  11.5 us (10%)
  local copies, waits for them, and re-layouts  3.47 us (3%)
  other arithmetic  2.93 us (3%)
    ppermute x8, waiting for transfers between devices, swapped(): return lax.ppermute(array, axis, [(i, i ^ bit) for i in range(peers)])  30.2 us
    ppermute x8, starting transfers between devices, swapped(): return lax.ppermute(array, axis, [(i, i ^ bit) for i in range(peers)])  13.8 us
    all_to_all x1, starting transfers between devices, shards(): lax.all_to_all(jnp.broadcast_to(own[None], (owners, *own.shape)), BLK, 0,...  11.7 us
    all_to_all x1, blocking collectives, shards(): parts = lax.all_to_all(parts.astype(F16), 'rep', 0, 0, tiled=True)  11.5 us
    pallas_call x1, Pallas kernels, shards(): pl.pallas_call(contract_kernel, out_shape=VMEM((reps, named * width + SUB...  11 us
    all_to_all x1, waiting for transfers between devices, shards(): chosen = lax.all_to_all(chosen, 'rep', 0, 0, tiled=True)  6.51 us
    all_to_all x1, starting transfers between devices, shards(): arrived = lax.all_to_all(scaled.astype(F16), BLK, 0, 0, tiled=True)  5.57 us
    all_to_all x1, waiting for transfers between devices, shards(): lax.all_to_all(jnp.broadcast_to(own[None], (owners, *own.shape)), BLK, 0,...  4.74 us
  transfers between devices with their start and end apart: 11, of which 10 were waited for; matrix products, arithmetic and copies ran while one was open for 2% of the time, Pallas kernels for 0%

profile of v6, /device:TPU:8, one launch (start us, length us, event | category | flops | bytes accessed | tf_op | source)
XLA Modules:
  0.0 109.3 jit_solution(17235374337056093525)
XLA Ops:
  0.0 0.0 copy-start
  0.0 0.7 copy-done
  0.7 0.9 broadcast_in_dim.10
  1.6 11.7 %all-to-all-start = ((bf16[32,2,32,128]{3,2,1,0:T(8,128)(2,1)}), bf16[32,2,32,128]{3,2,1,0:T(8,128)(2,1)S(1)}, u32[]{:S(2)}, u32[]{:S(2)}) async-start(bf16[32,2,32,128]{3,2,1,0:T(8,128)(2,1)} %broadcast_in_dim.10), calls=%async_computation | async-start | bytes 1048576 | tf_op jit(solution)/shard_map/all_to_all | solution.py:249
  13.3 0.7 convert_element_type.33
  14.0 0.1 convert_element_type.34
  14.1 0.1 collective-permute-start
  14.2 1.2 %collective-permute-done = bf16[1,80,128]{2,1,0:T(8,128)(2,1)S(1)} collective-permute-done((bf16[1,80,128]{2,1,0:T(8,128)(2,1)S(1)}, bf16[1,80,128]{2,1,0:T(8,128)(2,1)S(1)}, u32[]{:S(2)}, u32[]{:S(2)}) %collective-permute-start) | collective-permute-done | bytes 20512 | tf_op jit(solution)/shard_map/ppermute | solution.py:222
  15.4 1.5 %collective-permute-start.1 = (bf16[2,80,128]{2,1,0:T(8,128)(2,1)S(1)}, bf16[2,80,128]{2,1,0:T(8,128)(2,1)S(1)}, u32[]{:S(2)}, u32[]{:S(2)}) collective-permute-start(bf16[2,80,128]{2,1,0:T(8,128)(2,1)S(1)} %pad_maximum_fusion.2), channel_id=1, source_target_pairs={{0,2},{1,3},{2,0},{3,1},{4,6},{5,7},{6,4},{7,5},{8,10},{9,11},{10,... | collective-permute-start | bytes 122888 | tf_op jit(solution)/shard_map/ppermute | solution.py:222
  16.9 2.5 %collective-permute-done.1 = bf16[2,80,128]{2,1,0:T(8,128)(2,1)S(1)} collective-permute-done((bf16[2,80,128]{2,1,0:T(8,128)(2,1)S(1)}, bf16[2,80,128]{2,1,0:T(8,128)(2,1)S(1)}, u32[]{:S(2)}, u32[]{:S(2)}) %collective-permute-start.1) | collective-permute-done | bytes 40992 | tf_op jit(solution)/shard_map/ppermute | solution.py:222
  19.4 3.1 %collective-permute-start.2 = (bf16[4,80,128]{2,1,0:T(8,128)(2,1)S(1)}, bf16[4,80,128]{2,1,0:T(8,128)(2,1)S(1)}, u32[]{:S(2)}, u32[]{:S(2)}) collective-permute-start(bf16[4,80,128]{2,1,0:T(8,128)(2,1)S(1)} %pad_maximum_fusion.1), channel_id=1, source_target_pairs={{0,4},{1,5},{2,6},{3,7},{4,0},{5,1},{6,2},{7,3},{8,12},{9,13},{10,... | collective-permute-start | bytes 245768 | tf_op jit(solution)/shard_map/ppermute | solution.py:222
  22.5 2.9 %collective-permute-done.2 = bf16[4,80,128]{2,1,0:T(8,128)(2,1)S(1)} collective-permute-done((bf16[4,80,128]{2,1,0:T(8,128)(2,1)S(1)}, bf16[4,80,128]{2,1,0:T(8,128)(2,1)S(1)}, u32[]{:S(2)}, u32[]{:S(2)}) %collective-permute-start.2) | collective-permute-done | bytes 81952 | tf_op jit(solution)/shard_map/ppermute | solution.py:222
  25.4 4.7 %all-to-all-done = bf16[32,2,32,128]{3,2,1,0:T(8,128)(2,1)S(1)} async-done(((bf16[32,2,32,128]{3,2,1,0:T(8,128)(2,1)}), bf16[32,2,32,128]{3,2,1,0:T(8,128)(2,1)S(1)}, u32[]{:S(2)}, u32[]{:S(2)}) %all-to-all-start) | async-done | bytes 524320 | tf_op jit(solution)/shard_map/all_to_all | solution.py:249
  30.2 1.4 %select.8 = bf16[8,6,32,128]{3,2,1,0:T(8,128)(2,1)} custom-call(s32[8,6]{1,0:T(8,128)S(1)} %bitcast.32, s32[1]{0:T(128)} %bitcast.6.place, bf16[64,32,128]{2,1,0:T(8,128)(2,1)S(1)} %bitcast.29), custom_call_target="tpu_custom_call" | custom-call | tf_op jit(solution)/shard_map/select/pallas_call | solution.py:266
  31.6 4.3 %all-to-all-start.1 = ((bf16[8,6,32,128]{3,2,1,0:T(8,128)(2,1)}), bf16[8,6,32,128]{3,2,1,0:T(8,128)(2,1)S(1)}, u32[]{:S(2)}, u32[]{:S(2)}) async-start(bf16[8,6,32,128]{3,2,1,0:T(8,128)(2,1)} %select.8), calls=%async_computation.1 | async-start | bytes 786432 | tf_op jit(solution)/shard_map/all_to_all | solution.py:274
  36.5 0.0 copy-start.1
  36.5 1.7 %slice_bitcast_fusion.head = bf16[64,128,128]{2,1,0:T(8,128)(2,1)S(1)} fusion(bf16[2,128,128,128]{3,2,1,0:T(8,128)(2,1)} %x_far.1), kind=kLoop, calls=%fused_computation | loop fusion | bytes 4194304 | tf_op jit(solution)/shard_map/squeeze | solution.py:280
  38.3 6.5 %all-to-all-done.1.sel = bf16[8,6,32,128]{3,2,1,0:T(8,128)(2,1)S(1)} async-done(((bf16[8,6,32,128]{3,2,1,0:T(8,128)(2,1)}), bf16[8,6,32,128]{3,2,1,0:T(8,128)(2,1)S(1)}, u32[]{:S(2)}, u32[]{:S(2)}) %all-to-all-start.1) | async-done | bytes 393248 | tf_op jit(solution)/shard_map/all_to_all | solution.py:274
  44.8 0.0 copy-done.1
  44.8 11.0 %contract.1 = f32[8,200,128]{2,1,0:T(8,128)S(1)} custom-call(s32[2,3]{1,0:T(2,128)S(1)} %copy-done.1, s32[1]{0:T(128)S(6)} %copy.15.count, bf16[64,128,128]{2,1,0:T(8,128)(2,1)S(1)} %slice_bitcast_fusion.head, bf16[2,128,128,128]{3,2,1,0:T(8,128)(2,1)} %x_far.1, bf16[8,6,32,128]{3,2,1,0:T(8,128)(2,1)S(1)} %all-to-all-done.1.sel), custom_call_target="tpu_custom_call" | custom-call | tf_op jit(solution)/shard_map/contract/pallas_call | solution.py:281
  55.8 0.1 convert_element_type.37
  55.8 11.5 %all_to_all.20 = f16[8,200,128]{2,1,0:T(8,128)(2,1)S(1)} all-to-all(f16[8,200,128]{2,1,0:T(8,128)(2,1)S(1)} %convert_element_type.37), channel_id=1, replica_groups=mesh['blk_0'=8,'blk_1'=4,'rep'=8] {'rep'}, dimensions={0} | all-to-all | bytes 819200 | tf_op jit(solution)/shard_map/all_to_all | solution.py:305
  67.3 0.1 convert_element_type.38.parts
  67.4 1.1 scatter.1
  68.5 0.9 convert_element_type.39
  69.3 5.6 %all-to-all-start.3 = ((f16[32,72,128]{2,1,0:T(8,128)(2,1)}), f16[32,72,128]{2,1,0:T(8,128)(2,1)S(1)}, u32[]{:S(2)}, u32[]{:S(2)}) async-start(f16[32,72,128]{2,1,0:T(8,128)(2,1)} %convert_element_type.39), calls=%async_computation.3 | async-start | bytes 1179648 | tf_op jit(solution)/shard_map/all_to_all | solution.py:328
  75.0 0.1 gram.1
  75.1 0.3 collective-permute-start.3
  75.4 4.0 %collective-permute-done.3 = f32[32,256]{1,0:T(8,128)S(1)} collective-permute-done((f32[32,256]{1,0:T(8,128)S(1)}, f32[32,256]{1,0:T(8,128)S(1)}, u32[]{:S(2)}, u32[]{:S(2)}) %collective-permute-start.3) | collective-permute-done | bytes 32800 | tf_op jit(solution)/shard_map/ppermute | solution.py:222
  79.4 2.1 %collective-permute-start.4 = (f32[32,256]{1,0:T(8,128)S(1)}, f32[32,256]{1,0:T(8,128)S(1)}, u32[]{:S(2)}, u32[]{:S(2)}) collective-permute-start(f32[32,256]{1,0:T(8,128)S(1)} %add.17), channel_id=1, source_target_pairs={{0,64},{32,96},{64,0},{96,32},{128,192},{160,224},{192,128},{224,1... | collective-permute-start | bytes 98312 | tf_op jit(solution)/shard_map/ppermute | solution.py:222
  81.5 9.2 %collective-permute-done.4 = f32[32,256]{1,0:T(8,128)S(1)} collective-permute-done((f32[32,256]{1,0:T(8,128)S(1)}, f32[32,256]{1,0:T(8,128)S(1)}, u32[]{:S(2)}, u32[]{:S(2)}) %collective-permute-start.4) | collective-permute-done | bytes 32800 | tf_op jit(solution)/shard_map/ppermute | solution.py:222
  90.7 0.0 collective-permute-start.5
  90.7 3.9 %collective-permute-done.5 = f32[32,256]{1,0:T(8,128)S(1)} collective-permute-done((f32[32,256]{1,0:T(8,128)S(1)}, f32[32,256]{1,0:T(8,128)S(1)}, u32[]{:S(2)}, u32[]{:S(2)}) %collective-permute-start.5) | collective-permute-done | bytes 32800 | tf_op jit(solution)/shard_map/ppermute | solution.py:222
  94.6 4.5 %collective-permute-start.6 = (f32[32,256]{1,0:T(8,128)S(1)}, f32[32,256]{1,0:T(8,128)S(1)}, u32[]{:S(2)}, u32[]{:S(2)}) collective-permute-start(f32[32,256]{1,0:T(8,128)S(1)} %add.19), channel_id=1, source_target_pairs={{0,128},{32,160},{64,192},{96,224},{128,0},{160,32},{192,64},{224,... | collective-permute-start | bytes 98312 | tf_op jit(solution)/shard_map/ppermute | solution.py:222
  99.1 3.4 %collective-permute-done.6 = f32[32,256]{1,0:T(8,128)S(1)} collective-permute-done((f32[32,256]{1,0:T(8,128)S(1)}, f32[32,256]{1,0:T(8,128)S(1)}, u32[]{:S(2)}, u32[]{:S(2)}) %collective-permute-start.6) | collective-permute-done | bytes 32800 | tf_op jit(solution)/shard_map/ppermute | solution.py:222
  102.5 2.3 %collective-permute-start.7 = (f32[32,256]{1,0:T(8,128)S(1)}, f32[32,256]{1,0:T(8,128)S(1)}, u32[]{:S(2)}, u32[]{:S(2)}) collective-permute-start(f32[32,256]{1,0:T(8,128)S(1)} %add.20), channel_id=1, source_target_pairs={{0,16},{8,24},{16,0},{24,8},{1,17},{9,25},{17,1},{25,9},{2,18},{10... | collective-permute-start | bytes 98312 | tf_op jit(solution)/shard_map/ppermute | solution.py:222
  104.8 3.1 %collective-permute-done.7 = f32[32,256]{1,0:T(8,128)S(1)} collective-permute-done((f32[32,256]{1,0:T(8,128)S(1)}, f32[32,256]{1,0:T(8,128)S(1)}, u32[]{:S(2)}, u32[]{:S(2)}) %collective-permute-start.7) | collective-permute-done | bytes 32800 | tf_op jit(solution)/shard_map/ppermute | solution.py:222
  107.9 0.2 fit.1
  108.1 0.0 all-to-all-done.3
  108.1 0.1 convert_element_type.40
  108.2 0.3 fusion.6
  108.5 0.1 fusion
  108.6 0.6 bitcast_bitcast_fusion
  (12 shorter events, 0.1 us)
Async XLA Ops:
  0.0 0.7 copy-start
  1.6 28.5 %all-to-all-start = ((bf16[32,2,32,128]{3,2,1,0:T(8,128)(2,1)}), bf16[32,2,32,128]{3,2,1,0:T(8,128)(2,1)S(1)}, u32[]{:S(2)}, u32[]{:S(2)}) async-start(bf16[32,2,32,128]{3,2,1,0:T(8,128)(2,1)} %broadcast_in_dim.10), calls=%async_computation | async-start | bytes 1048576 | tf_op jit(solution)/shard_map/all_to_all | solution.py:249
  14.1 1.2 %collective-permute-start = (bf16[1,80,128]{2,1,0:T(8,128)(2,1)S(1)}, bf16[1,80,128]{2,1,0:T(8,128)(2,1)S(1)}, u32[]{:S(2)}, u32[]{:S(2)}) collective-permute-start(bf16[1,80,128]{2,1,0:T(8,128)(2,1)S(1)} %fusion.3), channel_id=1, source_target_pairs={{0,1},{1,0},{2,3},{3,2},{4,5},{5,4},{6,7},{7,6},{8,9},{9,8},{10,11... | collective-permute-start | bytes 61448 | tf_op jit(solution)/shard_map/ppermute | solution.py:222
  15.4 4.0 %collective-permute-start.1 = (bf16[2,80,128]{2,1,0:T(8,128)(2,1)S(1)}, bf16[2,80,128]{2,1,0:T(8,128)(2,1)S(1)}, u32[]{:S(2)}, u32[]{:S(2)}) collective-permute-start(bf16[2,80,128]{2,1,0:T(8,128)(2,1)S(1)} %pad_maximum_fusion.2), channel_id=1, source_target_pairs={{0,2},{1,3},{2,0},{3,1},{4,6},{5,7},{6,4},{7,5},{8,10},{9,11},{10,... | collective-permute-start | bytes 122888 | tf_op jit(solution)/shard_map/ppermute | solution.py:222
  19.4 6.0 %collective-permute-start.2 = (bf16[4,80,128]{2,1,0:T(8,128)(2,1)S(1)}, bf16[4,80,128]{2,1,0:T(8,128)(2,1)S(1)}, u32[]{:S(2)}, u32[]{:S(2)}) collective-permute-start(bf16[4,80,128]{2,1,0:T(8,128)(2,1)S(1)} %pad_maximum_fusion.1), channel_id=1, source_target_pairs={{0,4},{1,5},{2,6},{3,7},{4,0},{5,1},{6,2},{7,3},{8,12},{9,13},{10,... | collective-permute-start | bytes 245768 | tf_op jit(solution)/shard_map/ppermute | solution.py:222
  31.6 13.2 %all-to-all-start.1 = ((bf16[8,6,32,128]{3,2,1,0:T(8,128)(2,1)}), bf16[8,6,32,128]{3,2,1,0:T(8,128)(2,1)S(1)}, u32[]{:S(2)}, u32[]{:S(2)}) async-start(bf16[8,6,32,128]{3,2,1,0:T(8,128)(2,1)} %select.8), calls=%async_computation.1 | async-start | bytes 786432 | tf_op jit(solution)/shard_map/all_to_all | solution.py:274
  36.5 8.3 %copy-start.1 = (s32[2,3]{1,0:T(2,128)S(1)}, s32[2,3]{1,0:T(2,128)}, u32[]{:S(2)}) copy-start(s32[2,3]{1,0:T(2,128)} %triples.1) | copy-start | bytes 76
  69.3 38.7 %all-to-all-start.3 = ((f16[32,72,128]{2,1,0:T(8,128)(2,1)}), f16[32,72,128]{2,1,0:T(8,128)(2,1)S(1)}, u32[]{:S(2)}, u32[]{:S(2)}) async-start(f16[32,72,128]{2,1,0:T(8,128)(2,1)} %convert_element_type.39), calls=%async_computation.3 | async-start | bytes 1179648 | tf_op jit(solution)/shard_map/all_to_all | solution.py:328
  75.1 4.3 %collective-permute-start.3 = (f32[32,256]{1,0:T(8,128)S(1)}, f32[32,256]{1,0:T(8,128)S(1)}, u32[]{:S(2)}, u32[]{:S(2)}) collective-permute-start(f32[32,256]{1,0:T(8,128)S(1)} %gram.1), channel_id=1, source_target_pairs={{0,8},{8,0},{16,24},{24,16},{1,9},{9,1},{17,25},{25,17},{2,10},{10... | collective-permute-start | bytes 98312 | tf_op jit(solution)/shard_map/ppermute | solution.py:222
  79.4 11.3 %collective-permute-start.4 = (f32[32,256]{1,0:T(8,128)S(1)}, f32[32,256]{1,0:T(8,128)S(1)}, u32[]{:S(2)}, u32[]{:S(2)}) collective-permute-start(f32[32,256]{1,0:T(8,128)S(1)} %add.17), channel_id=1, source_target_pairs={{0,64},{32,96},{64,0},{96,32},{128,192},{160,224},{192,128},{224,1... | collective-permute-start | bytes 98312 | tf_op jit(solution)/shard_map/ppermute | solution.py:222
  90.7 3.9 %collective-permute-start.5 = (f32[32,256]{1,0:T(8,128)S(1)}, f32[32,256]{1,0:T(8,128)S(1)}, u32[]{:S(2)}, u32[]{:S(2)}) collective-permute-start(f32[32,256]{1,0:T(8,128)S(1)} %add.18), channel_id=1, source_target_pairs={{0,32},{32,0},{64,96},{96,64},{128,160},{160,128},{192,224},{224,1... | collective-permute-start | bytes 98312 | tf_op jit(solution)/shard_map/ppermute | solution.py:222
  94.6 7.8 %collective-permute-start.6 = (f32[32,256]{1,0:T(8,128)S(1)}, f32[32,256]{1,0:T(8,128)S(1)}, u32[]{:S(2)}, u32[]{:S(2)}) collective-permute-start(f32[32,256]{1,0:T(8,128)S(1)} %add.19), channel_id=1, source_target_pairs={{0,128},{32,160},{64,192},{96,224},{128,0},{160,32},{192,64},{224,... | collective-permute-start | bytes 98312 | tf_op jit(solution)/shard_map/ppermute | solution.py:222
  102.5 5.4 %collective-permute-start.7 = (f32[32,256]{1,0:T(8,128)S(1)}, f32[32,256]{1,0:T(8,128)S(1)}, u32[]{:S(2)}, u32[]{:S(2)}) collective-permute-start(f32[32,256]{1,0:T(8,128)S(1)} %add.20), channel_id=1, source_target_pairs={{0,16},{8,24},{16,0},{24,8},{1,17},{9,25},{17,1},{25,9},{2,18},{10... | collective-permute-start | bytes 98312 | tf_op jit(solution)/shard_map/ppermute | solution.py:222
